TPU v7x, 32 devices: a whole 2x2x4 slice. The times are simulated.
32 devices in a mesh: wide: 8 (over z, y), narrow: 4 (over x, core).
Axes of the slice: x: 2, y: 2, z: 4, core: 2. Of those that a mesh axis runs over, the one named last changes fastest.
Arguments:
- superheat_excess: float32 [32, 512, 512], P('wide', 'narrow'), may hold values from -6 to 6
- liquid_indicator: int32 [32, 512, 512], P('wide', 'narrow'), may hold values from 0 to 1, as said below
- group_patch_listing_table: int32 [8, 4, 16], P('wide', 'narrow'), may hold values from -1 to 31, as said below
- source_smearing_factors_north: float32 [16, 16], replicated, may hold values from 0 to 2, as said below
- source_smearing_factors_east: float32 [128, 128], replicated, may hold values from 0 to 2, as said below
Outputs:
- temperature_next: float32 [32, 512, 512], P('wide', 'narrow')
- pressure: float32 [32, 512, 512], P('wide', 'narrow')
- residual: float32 [32, 512, 512], P('wide', 'narrow')
Inputs may be any that keep to these rules, and one draw needn't show every extreme that they name: In each row group_patch_listing_table[w, n] the listed tile numbers come first and are distinct, the remaining entries are -1. A row lists 1 to 16 tiles; for every w the rows n < 4 list exactly 32 tiles together, and one of them lists 16. `liquid_indicator`: phase is 1 in every cell outside the listed tiles. `source_smearing_factors_north`: the identity plus entries drawn in 0 to 1.2 / 16. `source_smearing_factors_east`: the identity plus entries drawn in 0 to 1.2 / 128.
All inputs are finite; a program needn't handle non-finite values.
Results may differ from a plain program's by a relative error of at most 0.0003.
Values sent between devices are 32-bit elements; how exact they have to be, the bound alone decides.
No kernel may reach another device: no remote copies, remote signals or barrier semaphores. Data moves between devices by JAX's collectives and lax.ppermute only.
A program may use at most 64 MiB of HBM per device.

v0:
```python
import math

import jax
import jax.numpy as jnp
from jax import lax
from jax.sharding import PartitionSpec as P

ITERS = 3


conduct_liquid = 1.0
conduct_vapor = 0.4
diffusion = 0.06
mobility_liquid = 1.0
mobility_vapor = 4.0
expansion = 0.3
compress = 0.01
highest = lax.Precision.HIGHEST


def with_halo(cells, sides, width):
    for axis, dim in sides:
        count = lax.axis_size(axis)
        ends = count - 1
        head = lax.slice_in_dim(cells, 0, width, axis=dim)
        tail = lax.slice_in_dim(cells, cells.shape[dim] - width, cells.shape[dim], axis=dim)
        cells = jnp.concatenate(
            [
                lax.ppermute(tail, axis, [(i, (i + 1) % count) for i in range(ends)]),
                cells,
                lax.ppermute(head, axis, [((i + 1) % count, i) for i in range(ends)]),
            ],
            axis=dim,
        )
    return cells


def centre(padded):
    return padded[1:-1, 1:-1, 1:-1]


def neighbours(padded):
    return [
        padded[2:, 1:-1, 1:-1],
        padded[:-2, 1:-1, 1:-1],
        padded[1:-1, 2:, 1:-1],
        padded[1:-1, :-2, 1:-1],
        padded[1:-1, 1:-1, 2:],
        padded[1:-1, 1:-1, :-2],
    ]


def heat_advance(temp_pad, liquid_indicator_haloed, inner_region_haloed):
    current = centre(temp_pad)
    phases = centre(liquid_indicator_haloed)
    conduct = jnp.where(phases > 0.5, conduct_liquid, conduct_vapor)
    flux = jnp.zeros_like(current)
    faces = jnp.zeros_like(current)
    for near_temp, near_phase, near_inside in zip(
        neighbours(temp_pad), neighbours(liquid_indicator_haloed), neighbours(inner_region_haloed)
    ):
        differ = jnp.abs(near_phase - phases) > 0.5
        flux = flux + near_inside * jnp.where(differ, -2.0 * current, near_temp - current)
        faces = faces + near_inside * jnp.where(differ, 1.0, 0.0)
    heated_values = current + diffusion * conduct * flux
    vaporised_amount = 2.0 * conduct * faces * heated_values
    return (heated_values, vaporised_amount)


def face_weights(liquid_indicator_haloed, inner_region_haloed):
    mobility = jnp.where(liquid_indicator_haloed > 0.5, mobility_liquid, mobility_vapor)
    own = centre(mobility)
    return [
        near_inside * 0.5 * (own + near_mob)
        for near_inside, near_mob in zip(neighbours(inner_region_haloed), neighbours(mobility))
    ]


def apply_operator(field_pad, weights):
    field = centre(field_pad)
    total = compress * field
    for weight, near in zip(weights, neighbours(field_pad)):
        total = total + weight * (field - near)
    return total


def smear_tiles(tiles, source_smearing_factors_north, source_smearing_factors_east):
    across = jnp.einsum("...bc,dc->...bd", tiles, source_smearing_factors_east, precision=highest)
    return expansion * jnp.einsum(
        "ab,...bd->...ad", source_smearing_factors_north, across, precision=highest
    )


def cosine_rows(extent, klength, clength):
    waves = jnp.arange(klength, dtype=jnp.int32)
    centres = 2 * jnp.arange(clength, dtype=jnp.int32) + 1
    turns = waves[:, None] * centres[None, :] % (4 * extent)
    angles = 2.0 * math.pi / (4 * extent) * turns.astype(jnp.float32)
    scales = jnp.where(waves == 0, math.sqrt(1.0 / extent), math.sqrt(2.0 / extent)).astype(
        jnp.float32
    )
    return scales[:, None] * jnp.cos(angles)


def eigen(extent, first, length):
    waves = (first + jnp.arange(length, dtype=jnp.int32)).astype(jnp.float32)
    return 4.0 * jnp.sin(waves * (math.pi / (2 * extent))) ** 2


def inside_range(first, length, limit):
    places = first + jnp.arange(length, dtype=jnp.int32)
    return jnp.logical_and(places >= 0, places < limit).astype(jnp.float32)


def padded_field(field):
    rimmed = with_halo(field, (("wide", 0), ("narrow", 1)), 1)
    return jnp.pad(rimmed, ((0, 0), (0, 0), (1, 1)))


def inner(first_field, second_field):
    return lax.psum(jnp.sum(first_field * second_field), ("wide", "narrow"))


def on_device(
    superheat_excess,
    liquid_indicator,
    group_patch_listing_table,
    source_smearing_factors_north,
    source_smearing_factors_east,
):
    sheet_thickness, north_line_total, patch_span_east = superheat_excess.shape
    wide_count = lax.axis_size("wide")
    lanes = lax.axis_size("narrow")
    wide_index = lax.axis_index("wide")
    lane_index = lax.axis_index("narrow")
    total_y = north_line_total * lanes
    total_z = sheet_thickness * wide_count
    gathered_patches = jnp.stack([superheat_excess, liquid_indicator.astype(jnp.float32)])
    rimmed = with_halo(gathered_patches, (("wide", 1), ("narrow", 2)), 1)
    rimmed = jnp.pad(rimmed, ((0, 0), (0, 0), (0, 0), (1, 1)))
    z_inside = inside_range(wide_index * sheet_thickness - 1, sheet_thickness + 2, total_z)
    y_inside = inside_range(lane_index * north_line_total - 1, north_line_total + 2, total_y)
    x_inside = inside_range(-1, patch_span_east + 2, patch_span_east)
    inner_region_haloed = (
        z_inside[:, None, None] * y_inside[None, :, None] * x_inside[None, None, :]
    )
    heated_values, vaporised_amount = heat_advance(rimmed[0], rimmed[1], inner_region_haloed)
    flat_ids = group_patch_listing_table.reshape(-1)
    most = flat_ids.shape[0]
    size_y = source_smearing_factors_north.shape[0]
    size_x = source_smearing_factors_east.shape[0]
    tiles_y = north_line_total // size_y
    tiles_x = patch_span_east // size_x
    count_tiles = tiles_y * tiles_x
    blocks = vaporised_amount.reshape(sheet_thickness, tiles_y, size_y, tiles_x, size_x).transpose(
        1, 3, 0, 2, 4
    )
    blocks = blocks.reshape(count_tiles, sheet_thickness * size_y * size_x)
    listed = flat_ids >= 0
    numbers = jnp.arange(count_tiles, dtype=jnp.int32)
    choose = jnp.logical_and(flat_ids[:, None] == numbers[None, :], listed[:, None]).astype(
        jnp.float32
    )
    picked = jnp.dot(choose, blocks, precision=highest)
    smeared = smear_tiles(
        picked.reshape(most, sheet_thickness, size_y, size_x),
        source_smearing_factors_north,
        source_smearing_factors_east,
    ).reshape(most, -1)
    sourced = jnp.dot(choose.T, smeared, precision=highest)
    source = sourced.reshape(tiles_y, tiles_x, sheet_thickness, size_y, size_x).transpose(
        2, 0, 3, 1, 4
    )
    source = source.reshape(sheet_thickness, north_line_total, patch_span_east)
    table_x = cosine_rows(patch_span_east, patch_span_east, patch_span_east)
    table_z = cosine_rows(total_z, total_z, total_z)
    eigen_z = eigen(total_z, 0, total_z)
    table_y = cosine_rows(total_y, total_y, total_y).reshape(total_y, lanes, north_line_total)
    table_zw = table_z.reshape(total_z, wide_count, sheet_thickness)
    part_k = patch_span_east // (wide_count * lanes)
    eigen_y = eigen(total_y, 0, total_y)
    eigen_x = eigen(patch_span_east, (wide_index * lanes + lane_index) * part_k, part_k)

    def precondition(remainder):
        spectrum = jnp.einsum("zyx,kx->zyk", remainder, table_x, precision=highest)
        planes = lax.all_to_all(
            spectrum[None], ("wide", "narrow"), split_axis=3, concat_axis=0, tiled=True
        )
        planes = planes.reshape(wide_count, lanes, sheet_thickness, north_line_total, part_k)
        planes = jnp.einsum("wnzyk,mwz->mnyk", planes, table_zw, precision=highest)
        planes = jnp.einsum("mnyk,lny->mlk", planes, table_y, precision=highest)
        denom = eigen_z[:, None, None] + eigen_y[None, :, None] + eigen_x[None, None, :] + compress
        planes = jnp.einsum("mlk,lny->mnyk", planes / denom, table_y, precision=highest)
        planes = jnp.einsum("mnyk,mwz->wnzyk", planes, table_zw, precision=highest)
        planes = planes.reshape(wide_count * lanes, sheet_thickness, north_line_total, part_k)
        slabs = lax.all_to_all(planes, ("wide", "narrow"), split_axis=0, concat_axis=3, tiled=True)
        return jnp.einsum("zyk,kx->zyx", slabs[0], table_x, precision=highest)

    weights = face_weights(rimmed[1], inner_region_haloed)
    pressure = jnp.zeros_like(source)
    residual = source
    search = precondition(residual)
    aligned = inner(residual, search)
    direction = search
    for iteration in range(ITERS):
        image = apply_operator(padded_field(direction), weights)
        alpha = aligned / lax.psum(jnp.sum(direction * image), ("wide", "narrow"))
        pressure = pressure + alpha * direction
        residual = residual - alpha * image
        if iteration + 1 < ITERS:
            search = precondition(residual)
            renewed = inner(residual, search)
            direction = search + renewed / aligned * direction
            aligned = renewed
    return (heated_values, pressure, residual)


def solution(mesh):
    placed = (
        P("wide", "narrow", None),
        P("wide", "narrow", None),
        P("wide", "narrow", None),
        P(),
        P(),
    )
    return jax.shard_map(
        on_device,
        mesh=mesh,
        in_specs=placed,
        out_specs=(P("wide", "narrow", None), P("wide", "narrow", None), P("wide", "narrow", None)),
        check_vma=False,
    )
```

profile of v0, /device:TPU:0, one launch (start us, length us, event | category | flops | bytes accessed | tf_op | source)
XLA Modules:
  0.0 652.1 jit_solution(15787358940810904846)
XLA Ops:
  3.3 5.7 collective-permute-start
  10.6 20.2 %collective-permute-done = f32[2,1,128,512]{3,2,1,0:T(8,128)} collective-permute-done((f32[2,1,128,512]{3,2,1,0:T(8,128)}, f32[2,1,128,512]{3,2,1,0:T(8,128)}, u32[]{:S(2)}, u32[]{:S(2)}) %collective-permute-start) | collective-permute-done | bytes 524320 | tf_op jit(solution)/shard_map/ppermute | solution.py:29
  46.3 4.9 fusion.5
  63.4 17.8 %convolution_bitcast_fusion.15 = f32[1,4,128,512]{3,2,1,0:T(8,128)} fusion(f32[4,128,512]{2,1,0:T(8,128)S(1)} %reshape.309, s32[512]{0:T(512)S(1)} %multiply_add_fusion.3, f32[512]{0:T(512)S(1)} %fusion.269), kind=kOutput, calls=%fused_computation.49 | convolution fusion | flops 1614544896 | bytes 2101248 | tf_op jit(solution)/shard_map/zyx,kx->zyk/dot_general | solution.py:185
  83.7 8.0 %all-to-all-start = ((f32[1,4,128,512]{2,1,0,3:T(4,128)}), f32[1,4,128,512]{2,1,0,3:T(4,128)S(1)}, u32[]{:S(2)}, u32[]{:S(2)}) async-start(f32[1,4,128,512]{2,1,0,3:T(4,128)} %copy.56), calls=%async_computation | async-start | bytes 2097152 | tf_op jit(solution)/shard_map/all_to_all | solution.py:186
  91.9 25.9 %all-to-all-done = f32[1,4,128,512]{2,1,0,3:T(4,128)S(1)} async-done(((f32[1,4,128,512]{2,1,0,3:T(4,128)}), f32[1,4,128,512]{2,1,0,3:T(4,128)S(1)}, u32[]{:S(2)}, u32[]{:S(2)}) %all-to-all-start) | async-done | bytes 1048608 | tf_op jit(solution)/shard_map/all_to_all | solution.py:186
  119.7 6.4 fusion.118
  126.0 6.6 %convolution_bitcast_fusion.12 = f32[32,4,128,16,1]{2,0,3,1,4:T(8,128)S(1)} fusion(f32[32,512,16]{1,2,0:T(8,128)S(1)} %fusion.118, s32[4,128]{1,0:T(4,128)S(1)} %multiply_add_fusion.4, f32[512]{0:T(512)S(1)} %fusion.269), kind=kOutput, calls=%fused_computation.46 | convolution fusion | flops 1614544896 | bytes 2101248 | tf_op jit(solution)/shard_map/mlk,lny->mnyk/dot_general | solution.py:193
  134.1 29.6 %all_to_all.90 = f32[32,4,128,16]{2,3,1,0:T(8,128)S(1)} all-to-all(f32[32,4,128,16]{2,3,1,0:T(8,128)S(1)} %bitcast.220), channel_id=1, replica_groups=mesh['wide'=8,'narrow'=4] {'wide','narrow'}, dimensions={0} | all-to-all | bytes 2097152 | tf_op jit(solution)/shard_map/all_to_all | solution.py:196
  163.8 5.8 fusion.131
  174.4 9.5 %collective-permute-done.5 = f32[1,128,512]{2,1,0:T(8,128)S(1)} collective-permute-done((f32[1,128,512]{2,1,0:T(8,128)S(1)}, f32[1,128,512]{2,1,0:T(8,128)S(1)}, u32[]{:S(2)}, u32[]{:S(2)}) %collective-permute-start.5) | collective-permute-done | bytes 262176 | tf_op jit(solution)/shard_map/ppermute | solution.py:29
  190.7 7.6 %multiply_reduce_fusion.4 = (f32[]{:T(128)}, f32[]{:T(128)}, f32[4,128,512]{2,1,0:T(8,128)}, f32[4,128,512]{2,1,0:T(8,128)}, f32[4,128,512]{2,1,0:T(8,128)}, /*i...) fusion(f32[4,128,512]{2,1,0:T(8,128)S(1)} %fusion.131, ...), kind=kLoop, calls=%fused_computation.228 | loop fusion | flops 12845054 | bytes 25714696 | tf_op jit(solution)/shard_map/reduce_sum | solution.py:207
  198.3 41.8 %all-reduce.4 = (f32[]{:T(128)}, f32[]{:T(128)}) all-reduce(f32[]{:T(128)} %get-tuple-element.4, f32[]{:T(128)} %get-tuple-element.3), channel_id=1, replica_groups=mesh['wide'=8,'narrow'=4] {'wide','narrow'}, use_global_device_ids=true, to_apply=%region_1.2 | all-reduce | flops 2 | bytes 16 | tf_op jit(solution)/shard_map/psum | solution.py:121
  243.3 6.8 %convolution_bitcast_fusion.10 = f32[1,4,128,512]{3,2,1,0:T(8,128)} fusion(f32[4,128,512]{2,1,0:T(8,128)S(1)} %multiply_subtract_fusion.2, s32[512]{0:T(512)S(1)} %multiply_add_fusion.3, f32[512]{0:T(512)S(1)} %fusion.269), kind=kOutput, calls=%fused_computation.44 | convolution fusion | flops 1614544896 | bytes 2101248 | tf_op jit(solution)/shard_map/zyx,kx->zyk/dot_general | solution.py:185
  251.7 31.3 %all_to_all.91 = f32[1,4,128,512]{2,1,0,3:T(4,128)S(1)} all-to-all(f32[1,4,128,512]{2,1,0,3:T(4,128)S(1)} %copy.65), channel_id=1, replica_groups=mesh['wide'=8,'narrow'=4] {'wide','narrow'}, dimensions={3} | all-to-all | bytes 2097152 | tf_op jit(solution)/shard_map/all_to_all | solution.py:186
  284.8 6.4 fusion.117
  291.2 6.6 %convolution_bitcast_fusion.7 = f32[32,4,128,16,1]{2,0,3,1,4:T(8,128)S(1)} fusion(f32[32,512,16]{1,2,0:T(8,128)S(1)} %fusion.117, s32[4,128]{1,0:T(4,128)S(1)} %multiply_add_fusion.4, f32[512]{0:T(512)S(1)} %fusion.269), kind=kOutput, calls=%fused_computation.41 | convolution fusion | flops 1614544896 | bytes 2101248 | tf_op jit(solution)/shard_map/mlk,lny->mnyk/dot_general | solution.py:193
  299.2 29.6 %all_to_all.92 = f32[32,4,128,16]{2,3,1,0:T(8,128)S(1)} all-to-all(f32[32,4,128,16]{2,3,1,0:T(8,128)S(1)} %bitcast.223), channel_id=1, replica_groups=mesh['wide'=8,'narrow'=4] {'wide','narrow'}, dimensions={0} | all-to-all | bytes 2097152 | tf_op jit(solution)/shard_map/all_to_all | solution.py:196
  328.9 6.6 %multiply_reduce_fusion.3 = (f32[]{:T(128)}, f32[4,128,512]{2,1,0:T(8,128)S(1)}) fusion(f32[4,128,512]{2,1,0:T(8,128)S(1)} %multiply_subtract_fusion.2, f32[4,128,512]{1,2,0:T(8,128)S(1)} %bitcast.231, s32[512]{0:T(512)S(1)} %multiply_add_fusion.3, f32[512]{0:T(512)S(1)} %fusion.269), kind=kOutput, calls=%fused_computation.226 | convolution fusion | flops 1615069184 | bytes 3149828 | tf_op jit(solution)/shard_map/zyk,kx->zyx/dot_general | solution.py:197
  335.5 38.7 %psum.44 = f32[]{:T(128)} all-reduce(f32[]{:T(128)} %get-tuple-element.45), channel_id=1, replica_groups=mesh['wide'=8,'narrow'=4] {'wide','narrow'}, use_global_device_ids=true, to_apply=%region_5.6 | all-reduce | flops 1 | bytes 8 | tf_op jit(solution)/shard_map/psum | solution.py:121
  375.8 4.6 collective-permute-start.9
  381.7 8.8 %collective-permute-done.9 = f32[1,128,512]{2,1,0:T(8,128)S(1)} collective-permute-done((f32[1,128,512]{2,1,0:T(8,128)S(1)}, f32[1,128,512]{2,1,0:T(8,128)S(1)}, u32[]{:S(2)}, u32[]{:S(2)}) %collective-permute-start.9) | collective-permute-done | bytes 262176 | tf_op jit(solution)/shard_map/ppermute | solution.py:29
  399.2 42.9 %psum.45 = f32[]{:T(128)} all-reduce(f32[]{:T(128)} %get-tuple-element.9), channel_id=1, replica_groups=mesh['wide'=8,'narrow'=4] {'wide','narrow'}, use_global_device_ids=true, to_apply=%region_7.8 | all-reduce | flops 1 | bytes 8 | tf_op jit(solution)/shard_map/psum | solution.py:207
  445.9 6.8 %convolution_bitcast_fusion.5 = f32[1,4,128,512]{3,2,1,0:T(8,128)} fusion(f32[4,128,512]{2,1,0:T(8,128)S(1)} %multiply_subtract_fusion.1, s32[512]{0:T(512)S(1)} %multiply_add_fusion.3, f32[512]{0:T(512)S(1)} %fusion.269), kind=kOutput, calls=%fused_computation.39 | convolution fusion | flops 1614544896 | bytes 2101248 | tf_op jit(solution)/shard_map/zyx,kx->zyk/dot_general | solution.py:185
  454.3 30.7 %all_to_all.93 = f32[1,4,128,512]{2,1,0,3:T(4,128)S(1)} all-to-all(f32[1,4,128,512]{2,1,0,3:T(4,128)S(1)} %copy.74), channel_id=1, replica_groups=mesh['wide'=8,'narrow'=4] {'wide','narrow'}, dimensions={3} | all-to-all | bytes 2097152 | tf_op jit(solution)/shard_map/all_to_all | solution.py:186
  486.7 6.4 fusion.116
  493.1 6.4 convolution_bitcast_fusion.2
  500.9 29.6 %all_to_all.94 = f32[32,4,128,16]{2,3,1,0:T(8,128)S(1)} all-to-all(f32[32,4,128,16]{2,3,1,0:T(8,128)S(1)} %bitcast.226), channel_id=1, replica_groups=mesh['wide'=8,'narrow'=4] {'wide','narrow'}, dimensions={0} | all-to-all | bytes 2097152 | tf_op jit(solution)/shard_map/all_to_all | solution.py:196
  530.7 7.5 %multiply_reduce_fusion.1 = (f32[]{:T(128)}, f32[4,128,512]{2,1,0:T(8,128)}) fusion(f32[4,128,512]{2,1,0:T(8,128)S(1)} %copy-done.22, f32[4,128,512]{1,2,0:T(8,128)S(1)} %bitcast.230, s32[512]{0:T(512)S(1)} %multiply_add_fusion.3, f32[512]{0:T(512)S(1)} %fusion.269), kind=kOutput, calls=%fused_computation.222 | convolution fusion | flops 1615069184 | bytes 3149828 | tf_op jit(solution)/shard_map/zyk,kx->zyx/dot_general | solution.py:197
  538.1 38.7 %psum.46 = f32[]{:T(128)} all-reduce(f32[]{:T(128)} %get-tuple-element.47), channel_id=1, replica_groups=mesh['wide'=8,'narrow'=4] {'wide','narrow'}, use_global_device_ids=true, to_apply=%region_9.10 | all-reduce | flops 1 | bytes 8 | tf_op jit(solution)/shard_map/psum | solution.py:121
  585.5 8.8 %collective-permute-done.13 = f32[1,128,512]{2,1,0:T(8,128)S(1)} collective-permute-done((f32[1,128,512]{2,1,0:T(8,128)S(1)}, f32[1,128,512]{2,1,0:T(8,128)S(1)}, u32[]{:S(2)}, u32[]{:S(2)}) %collective-permute-start.13) | collective-permute-done | bytes 262176 | tf_op jit(solution)/shard_map/ppermute | solution.py:29
  603.9 42.9 %psum.47 = f32[]{:T(128)} all-reduce(f32[]{:T(128)} %get-tuple-element.7), channel_id=1, replica_groups=mesh['wide'=8,'narrow'=4] {'wide','narrow'}, use_global_device_ids=true, to_apply=%region_11.12 | all-reduce | flops 1 | bytes 8 | tf_op jit(solution)/shard_map/psum | solution.py:207
  (145 shorter events, 93.5 us)
Async XLA Ops:
  0.6 56.9 %copy-start = (f32[128,128]{1,0:T(8,128)S(1)}, f32[128,128]{1,0:T(8,128)}, u32[]{:S(2)}) copy-start(f32[128,128]{1,0:T(8,128)} %param.9) | copy-start | bytes 196612
  2.1 8.2 %copy-start.24 = (s32[1,1,16]{2,1,0:T(1,128)S(1)}, s32[1,1,16]{2,1,0:T(1,128)}, u32[]{:S(2)}) copy-start(s32[1,1,16]{2,1,0:T(1,128)} %param.7) | copy-start | bytes 196
  3.3 27.6 %collective-permute-start = (f32[2,1,128,512]{3,2,1,0:T(8,128)}, f32[2,1,128,512]{3,2,1,0:T(8,128)}, u32[]{:S(2)}, u32[]{:S(2)}) collective-permute-start(f32[2,1,128,512]{3,2,1,0:T(8,128)} %get-tuple-element.24), channel_id=1, source_target_pairs={{0,4},{4,8},{8,12},{12,16},{16,20},{20,24},{24,28},{1,5},{5,9},{9,... | collective-permute-start | bytes 1572872 | tf_op jit(solution)/shard_map/ppermute | solution.py:29
  9.0 21.9 %collective-permute-start.1 = (f32[2,1,128,512]{3,2,1,0:T(8,128)}, f32[2,1,128,512]{3,2,1,0:T(8,128)}, u32[]{:S(2)}, u32[]{:S(2)}) collective-permute-start(f32[2,1,128,512]{3,2,1,0:T(8,128)} %get-tuple-element.25), channel_id=1, source_target_pairs={{4,0},{8,4},{12,8},{16,12},{20,16},{24,20},{28,24},{5,1},{9,5},{13... | collective-permute-start | bytes 1572872 | tf_op jit(solution)/shard_map/ppermute | solution.py:31
  10.6 27.3 %copy-start.5 = (f32[4,128,512]{2,1,0:T(8,128)S(1)}, f32[4,128,512]{2,1,0:T(8,128)}, u32[]{:S(2)}) copy-start(f32[4,128,512]{2,1,0:T(8,128)} %param.5) | copy-start | bytes 3145732
  31.9 2.6 collective-permute-start.2
  33.2 4.8 collective-permute-start.3
  63.3 17.8 %copy-start.18 = (f32[4,128,512]{2,1,0:T(8,128)}, f32[4,128,512]{2,1,0:T(8,128)S(1)}, u32[]{:S(2)}) copy-start(f32[4,128,512]{2,1,0:T(8,128)S(1)} %reshape.309) | copy-start | bytes 3145732
  83.7 34.2 %all-to-all-start = ((f32[1,4,128,512]{2,1,0,3:T(4,128)}), f32[1,4,128,512]{2,1,0,3:T(4,128)S(1)}, u32[]{:S(2)}, u32[]{:S(2)}) async-start(f32[1,4,128,512]{2,1,0,3:T(4,128)} %copy.56), calls=%async_computation | async-start | bytes 2097152 | tf_op jit(solution)/shard_map/all_to_all | solution.py:186
  163.8 22.7 %copy-start.3 = (f32[2,6,130,514]{3,2,1,0:T(8,128)S(1)}, f32[2,6,130,514]{3,2,1,0:T(8,128)}, u32[]{:S(2)}) copy-start(f32[2,6,130,514]{3,2,1,0:T(8,128)} %copy-done.2) | copy-start | bytes 9622084
  169.7 14.2 %collective-permute-start.5 = (f32[1,128,512]{2,1,0:T(8,128)S(1)}, f32[1,128,512]{2,1,0:T(8,128)S(1)}, u32[]{:S(2)}, u32[]{:S(2)}) collective-permute-start(f32[1,128,512]{2,1,0:T(8,128)S(1)} %get-tuple-element.43), channel_id=1, source_target_pairs={{0,4},{4,8},{8,12},{12,16},{16,20},{20,24},{24,28},{1,5},{5,9},{9,... | collective-permute-start | bytes 786440 | tf_op jit(solution)/shard_map/ppermute | solution.py:29
  173.1 10.8 %collective-permute-start.4 = (f32[1,128,512]{2,1,0:T(8,128)S(1)}, f32[1,128,512]{2,1,0:T(8,128)S(1)}, u32[]{:S(2)}, u32[]{:S(2)}) collective-permute-start(f32[1,128,512]{2,1,0:T(8,128)S(1)} %get-tuple-element.44), channel_id=1, source_target_pairs={{4,0},{8,4},{12,8},{16,12},{20,16},{24,20},{28,24},{5,1},{9,5},{13... | collective-permute-start | bytes 786440 | tf_op jit(solution)/shard_map/ppermute | solution.py:31
  183.9 2.8 collective-permute-start.7
  185.2 4.8 collective-permute-start.6
  243.3 85.7 %copy-start.20 = (f32[4,128,512]{2,1,0:T(8,128)}, f32[4,128,512]{2,1,0:T(8,128)S(1)}, u32[]{:S(2)}) copy-start(f32[4,128,512]{2,1,0:T(8,128)S(1)} %multiply_subtract_fusion.2) | copy-start | bytes 3145732
  375.7 21.2 %copy-start.16 = (f32[4,128,512]{2,1,0:T(8,128)S(1)}, f32[4,128,512]{2,1,0:T(8,128)}, u32[]{:S(2)}) copy-start(f32[4,128,512]{2,1,0:T(8,128)} %get-tuple-element.17) | copy-start | bytes 3145732
  375.8 14.7 %collective-permute-start.9 = (f32[1,128,512]{2,1,0:T(8,128)S(1)}, f32[1,128,512]{2,1,0:T(8,128)S(1)}, u32[]{:S(2)}, u32[]{:S(2)}) collective-permute-start(f32[1,128,512]{2,1,0:T(8,128)S(1)} %get-tuple-element.41), channel_id=1, source_target_pairs={{0,4},{4,8},{8,12},{12,16},{16,20},{20,24},{24,28},{1,5},{5,9},{9,... | collective-permute-start | bytes 786440 | tf_op jit(solution)/shard_map/ppermute | solution.py:29
  380.4 10.1 %collective-permute-start.8 = (f32[1,128,512]{2,1,0:T(8,128)S(1)}, f32[1,128,512]{2,1,0:T(8,128)S(1)}, u32[]{:S(2)}, u32[]{:S(2)}) collective-permute-start(f32[1,128,512]{2,1,0:T(8,128)S(1)} %get-tuple-element.42), channel_id=1, source_target_pairs={{4,0},{8,4},{12,8},{16,12},{20,16},{24,20},{28,24},{5,1},{9,5},{13... | collective-permute-start | bytes 786440 | tf_op jit(solution)/shard_map/ppermute | solution.py:31
  390.5 6.5 copy-start.12
  390.5 6.5 copy-start.14
  390.5 6.5 copy-start.6
  390.5 6.5 copy-start.8
  390.5 2.9 collective-permute-start.11
  392.1 4.1 collective-permute-start.10
  500.9 29.7 %copy-start.22 = (f32[4,128,512]{2,1,0:T(8,128)S(1)}, f32[4,128,512]{2,1,0:T(8,128)}, u32[]{:S(2)}) copy-start(f32[4,128,512]{2,1,0:T(8,128)} %copy-done.21) | copy-start | bytes 3145732
  578.1 22.6 %copy-start.17 = (f32[4,128,512]{2,1,0:T(8,128)S(1)}, f32[4,128,512]{2,1,0:T(8,128)}, u32[]{:S(2)}) copy-start(f32[4,128,512]{2,1,0:T(8,128)} %get-tuple-element.17) | copy-start | bytes 3145732
  579.7 14.6 %collective-permute-start.13 = (f32[1,128,512]{2,1,0:T(8,128)S(1)}, f32[1,128,512]{2,1,0:T(8,128)S(1)}, u32[]{:S(2)}, u32[]{:S(2)}) collective-permute-start(f32[1,128,512]{2,1,0:T(8,128)S(1)} %get-tuple-element.39), channel_id=1, source_target_pairs={{0,4},{4,8},{8,12},{12,16},{16,20},{20,24},{24,28},{1,5},{5,9},{9,... | collective-permute-start | bytes 786440 | tf_op jit(solution)/shard_map/ppermute | solution.py:29
  584.2 10.1 %collective-permute-start.12 = (f32[1,128,512]{2,1,0:T(8,128)S(1)}, f32[1,128,512]{2,1,0:T(8,128)S(1)}, u32[]{:S(2)}, u32[]{:S(2)}) collective-permute-start(f32[1,128,512]{2,1,0:T(8,128)S(1)} %get-tuple-element.40), channel_id=1, source_target_pairs={{4,0},{8,4},{12,8},{16,12},{20,16},{24,20},{28,24},{5,1},{9,5},{13... | collective-permute-start | bytes 786440 | tf_op jit(solution)/shard_map/ppermute | solution.py:31
  594.3 6.5 copy-start.13
  594.3 6.5 copy-start.15
  594.4 3.1 collective-permute-start.15
  595.9 4.1 collective-permute-start.14
  (10 other events, 41.1 us)
where the time goes:
time: 663 us; the launch traced here: 652 us
  blocking collectives  356 us (54%)
  matrix products  102 us (15%)
  waiting for transfers between devices  85.3 us (13%)
  starting transfers between devices  42.4 us (6%)
  other arithmetic  39 us (6%)
  local copies, waits for them, and re-layouts  19.1 us (3%)
  between operations  8.73 us (1%)
    psum x3, blocking collectives, inner(): return lax.psum(jnp.sum(first_field * second_field), ('wide', 'narrow'))  119 us
    all_to_all x3, blocking collectives, precondition(): lax.all_to_all(planes, ('wide', 'narrow'), split_axis=0, concat_axis=3, t...  88.9 us
    psum x2, blocking collectives, on_device(): alpha = aligned / lax.psum(jnp.sum(direction * image), ('wide', 'narrow'))  85.8 us
    all_to_all x2, blocking collectives, precondition(): lax.all_to_all(spectrum[None], ('wide', 'narrow'), split_axis=3, concat_a...  62 us
    ppermute x8, waiting for transfers between devices, with_halo(): lax.ppermute(tail, axis, [(i, (i + 1) % count) for i in range(ends)])  47.4 us
    dot_general x3, matrix products, precondition(): spectrum = jnp.einsum('zyx,kx->zyk', remainder, table_x, precision=highest)  31.3 us
    all_to_all x1, waiting for transfers between devices, precondition(): lax.all_to_all(spectrum[None], ('wide', 'narrow'), split_axis=3, concat_a...  25.9 us
    ppermute x8, starting transfers between devices, with_halo(): lax.ppermute(tail, axis, [(i, (i + 1) % count) for i in range(ends)])  23.8 us
  transfers between devices with their start and end apart: 17, of which 9 were waited for; matrix products, arithmetic and copies ran while one was open for 0% of the time, Pallas kernels for 0%

commit v1 on v0

v1 whole, which is shorter than its diff:
```python
import math

import jax
import jax.numpy as jnp
import numpy as np
from jax import lax
from jax.experimental import pallas as pl
from jax.experimental.pallas import tpu as pltpu
from jax.sharding import PartitionSpec as P

ITERS = 3

conduct_liquid = 1.0
conduct_vapor = 0.4
diffusion = 0.06
mobility_liquid = 1.0
mobility_vapor = 4.0
expansion = 0.3
compress = 0.01
highest = lax.Precision.HIGHEST
f32 = jnp.float32
LANES = 128
VMEM = pltpu.VMEM
ORDER = ("narrow", "wide")


def mat(a, b):
    return lax.dot_general(
        a, b, (((1,), (0,)), ((), ())), precision=highest, preferred_element_type=f32
    )


def mat_t(a, b):
    return lax.dot_general(
        a, b, (((1,), (1,)), ((), ())), precision=highest, preferred_element_type=f32
    )


def cosine(m):
    k = np.arange(m)[:, None]
    i = np.arange(m)[None, :]
    scale = np.where(k == 0, math.sqrt(1.0 / m), math.sqrt(2.0 / m))
    return scale * np.cos(np.pi * (k * (2 * i + 1) % (4 * m)) / (2 * m))


def eigen(m):
    return 4.0 * np.sin(np.pi * np.arange(m) / (2 * m)) ** 2


def tables(depth, rows, span, blocks):
    half = depth // 2
    c_z, c_r, c_x = cosine(depth), cosine(rows), cosine(span)
    order = np.concatenate([np.arange(0, depth, 2), np.arange(1, depth, 2)])
    forward = []
    for parity in range(2):
        c = c_z[parity::2, :half]
        forward.append(
            np.einsum("ky,mz->kmzy", c_r, c).reshape(rows * half, half * rows)
        )
    c_sorted = c_z[order]
    swap = np.zeros((2 * depth, 2 * depth))
    swap[:depth, :depth] = c_sorted.T
    swap[depth:, depth:] = c_sorted.T
    shift = eigen(depth)[order][:, None] + eigen(span)[None, :] + compress
    lam = eigen(rows)
    first, last = c_r[:, 0], c_r[:, rows - 1]
    den = lam[None, :, None] + shift[:, None, :]
    same = ((first**2)[None, :, None] / den).sum(1)
    cross = ((first * last)[None, :, None] / den).sum(1)
    m = np.arange(1, blocks)
    sine = np.zeros((blocks, blocks))
    sine[: blocks - 1, : blocks - 1] = math.sqrt(2.0 / blocks) * np.sin(
        np.pi * m[:, None] * m[None, :] / blocks
    )
    wave = np.zeros((blocks, 1))
    wave[: blocks - 1, 0] = 2.0 * np.cos(np.pi * m / blocks)
    return {
        "c_x": c_x.astype(np.float32),
        "forward": np.stack(forward).astype(np.float32),
        "inverse": np.stack([f.T for f in forward]).astype(np.float32),
        "swap": swap.astype(np.float32),
        "shift": shift.astype(np.float32),
        "lam": [float(v) for v in lam],
        "first": [float(v) for v in first],
        "last": [float(v) for v in last],
        "pair": np.stack([1.0 + 2.0 * same, cross], 1).astype(np.float32),
        "sine": sine.astype(np.float32),
        "wave": np.broadcast_to(wave, (blocks, LANES)).astype(np.float32).copy(),
    }


def call(body, outs, *args, smem=(), scratch=(), flops=1e9, name=None):
    specs = [
        pl.BlockSpec(memory_space=pltpu.SMEM if i in smem else VMEM) for i in range(len(args))
    ]
    return pl.pallas_call(
        body,
        out_shape=[jax.ShapeDtypeStruct(s, f32) for s in outs],
        in_specs=specs,
        out_specs=[pl.BlockSpec(memory_space=VMEM)] * len(outs),
        scratch_shapes=list(scratch),
        compiler_params=pltpu.CompilerParams(vmem_limit_bytes=40 * 2**20),
        cost_estimate=pl.CostEstimate(flops=int(flops), bytes_accessed=4 << 20, transcendentals=0),
        name=name,
    )(*args)


def step(count, aligned, body):
    if aligned:
        lax.fori_loop(0, count, lambda i, c: (body(i), c)[1], 0)
    else:
        for i in range(count):
            body(i)


def row_roll(x, up):
    n = x.shape[0]
    if n % 8 == 0:
        return pltpu.roll(x, n - 1 if up else 1, 0)
    if up:
        return jnp.concatenate([x[1:], x[:1]], 0)
    return jnp.concatenate([x[-1:], x[:-1]], 0)


def lane_roll(x, up):
    n = x.shape[1]
    return pltpu.roll(x, n - 1 if up else 1, 1)


def fold_lanes(x):
    total = x[:, :LANES]
    for i in range(1, x.shape[1] // LANES):
        total = total + x[:, i * LANES : (i + 1) * LANES]
    return jnp.sum(total, axis=0, keepdims=True)


def heat_body(dims, *refs):
    thick, north, span, size_y, size_x, most = dims
    (pos, table, temp, phase, zlo, zhi, ylo, yhi, smear_n, smear_e,
     heated, source, tp, pp, mass, mask) = refs
    tiles_y = north // size_y
    tiles_x = span // size_x
    w_first, w_last = pos[0] == 0, pos[1] == 0
    n_first, n_last = pos[2] == 0, pos[3] == 0
    for z in range(thick):
        tp[z + 1] = temp[z]
        pp[z + 1] = phase[z].astype(f32)
    tp[0] = jnp.where(w_first, temp[0], zlo[0])
    pp[0] = jnp.where(w_first, phase[0].astype(f32), zlo[1])
    tp[thick + 1] = jnp.where(w_last, temp[thick - 1], zhi[0])
    pp[thick + 1] = jnp.where(w_last, phase[thick - 1].astype(f32), zhi[1])
    row = lax.broadcasted_iota(jnp.int32, (tiles_y, span), 0)
    lane = lax.broadcasted_iota(jnp.int32, (tiles_y, span), 1)
    tile = row * tiles_x + lane // size_x
    hit = tile == table[0]
    for i in range(1, most):
        hit = jnp.logical_or(hit, tile == table[i])
    mask[...] = jnp.where(hit, expansion, 0.0)
    r = lax.broadcasted_iota(jnp.int32, (size_y, span), 0)
    c = lax.broadcasted_iota(jnp.int32, (size_y, span), 1)

    def plane(z):
        for yc in range(tiles_y):
            at = pl.ds(yc * size_y, size_y)
            t = tp[z + 1, at, :]
            p = pp[z + 1, at, :]

            def edge(ref, halo, k, y, wall, own):
                if 0 <= y < north:
                    return ref[z + 1, pl.ds(y, 1), :]
                return jnp.where(wall, own, halo[k, z])

            pairs = [
                (tp[z, at, :], pp[z, at, :]),
                (tp[z + 2, at, :], pp[z + 2, at, :]),
                (jnp.where(c == span - 1, t, lane_roll(t, True)),
                 jnp.where(c == span - 1, p, lane_roll(p, True))),
                (jnp.where(c == 0, t, lane_roll(t, False)),
                 jnp.where(c == 0, p, lane_roll(p, False))),
            ]
            y = (yc + 1) * size_y
            pairs.append((
                jnp.where(r == size_y - 1, edge(tp, yhi, 0, y, n_last, t[size_y - 1:]), row_roll(t, True)),
                jnp.where(r == size_y - 1, edge(pp, yhi, 1, y, n_last, p[size_y - 1:]), row_roll(p, True)),
            ))
            y = yc * size_y - 1
            pairs.append((
                jnp.where(r == 0, edge(tp, ylo, 0, y, n_first, t[:1]), row_roll(t, False)),
                jnp.where(r == 0, edge(pp, ylo, 1, y, n_first, p[:1]), row_roll(p, False)),
            ))
            flux = jnp.zeros_like(t)
            faces = jnp.zeros_like(t)
            for near_t, near_p in pairs:
                differ = near_p != p
                flux = flux + jnp.where(differ, -2.0 * t, near_t - t)
                faces = faces + jnp.where(differ, 1.0, 0.0)
            k = jnp.where(p > 0.5, conduct_liquid, conduct_vapor)
            value = t + diffusion * k * flux
            heated[z, at, :] = value
            mass[pl.ds(pl.multiple_of(z * north, north) + yc * size_y, size_y), :] = 2.0 * k * faces * value

    lax.fori_loop(0, thick, lambda z, carry: (plane(z), carry)[1], 0)
    for tx in range(tiles_x):
        at = slice(tx * size_x, (tx + 1) * size_x)
        mass[:, at] = mat_t(mass[:, at], smear_e[...])
    for z in range(thick):
        smeared = mat(smear_n[...], mass[z * north : (z + 1) * north, :])
        for yc in range(tiles_y):
            source[yc, z] = smeared[yc * size_y : (yc + 1) * size_y] * mask[yc : yc + 1, :]


def forward_body(dims, tab, field, fold, spec, fwd, c_x, shift, message, extra):
    depth, rows, span = dims
    half = depth // 2
    size = half * rows
    aligned = rows % 8 == 0
    for parity in range(2):
        for z in range(half):
            a = field[z * rows : (z + 1) * rows, :]
            b = field[(depth - 1 - z) * rows : (depth - z) * rows, :]
            fold[z * rows : (z + 1) * rows, :] = a + b if parity == 0 else a - b
        spec[parity * size : (parity + 1) * size, :] = mat_t(
            mat(fwd[parity], fold[:size, :]), c_x[...]
        )
    for parity in range(2):
        mu = shift[parity * half : (parity + 1) * half, :]
        low = jnp.zeros((half, span), f32)
        high = jnp.zeros((half, span), f32)
        for ky in range(rows):
            at = parity * size + ky * half
            g = spec[at : at + half, :] / (mu + tab["lam"][ky])
            low = low + tab["first"][ky] * g
            high = high + tab["last"][ky] * g
        for k in range(half):
            o = parity * half + k
            message[o, 0:1, :span] = low[k : k + 1]
            message[o, 0:1, span : 2 * span] = high[k : k + 1]
            message[o, 0:1, 2 * span :] = extra


def start_body(dims, tab, source, fwd, c_x, shift, spec, message, fold):
    forward_body(dims, tab, source, fold, spec, fwd, c_x, shift, message, jnp.zeros((1, LANES), f32))


def solve_body(dims, tab, first_call, blocks, *refs):
    depth, rows, span = dims
    half = depth // 2
    if first_call:
        (got, spec, shift, pair, sine, wave, h_new, message, low, high) = refs
    else:
        (got, spec, shift, pair, sine, wave, image_spec, h_old, rho,
         spec_new, h_new, message, alpha_out, low, high) = refs
    for j in range(blocks):
        low[j : j + 1, :] = got[j, 0:1, :span]
        high[j : j + 1, :] = got[j, 0:1, span : 2 * span]
    jump = high[...] - row_roll(low[...], True)
    r = lax.broadcasted_iota(jnp.int32, (blocks, span), 0)
    jump = jnp.where(r == blocks - 1, 0.0, jump)
    if not first_call:
        bottom = jnp.zeros((1, LANES), f32)
        for j in range(blocks):
            bottom = bottom + got[j, 0:1, 2 * span :]
        alpha = rho[...] / jnp.sum(bottom, axis=1, keepdims=True)
        alpha_out[...] = alpha
        alpha = alpha[:, :1]
        jump = h_old[...] - alpha * jump
    h_new[...] = jump
    scale = 1.0 / (pair[0:1, :] - wave[:, :1] * pair[1:2, :])
    q = mat(sine[...], mat(sine[...], jump) * scale)
    total = fold_lanes(q * jump) * -1.0
    acc = jnp.zeros((8, span), f32)
    for parity in range(2):
        mu = shift[parity * half : (parity + 1) * half, :]
        for ky in range(rows):
            at = parity * half * rows + ky * half
            s = spec[at : at + half, :]
            if not first_call:
                s = s - alpha * image_spec[at : at + half, :]
                spec_new[at : at + half, :] = s
            e = s * s / (mu + tab["lam"][ky])
            for i in range(half // 8):
                acc = acc + e[i * 8 : (i + 1) * 8]
    total = total + fold_lanes(acc)
    zero = jnp.zeros((1, span), f32)
    for j in range(blocks):
        message[j, 0:1, :span] = zero if j == 0 else q[j - 1 : j]
        message[j, 0:1, span : 2 * span] = q[j : j + 1]
        message[j, 0:1, 2 * span :] = total


def advance_body(dims, tab, first_call, last_call, blocks, *refs):
    depth, rows, span = dims
    half = depth // 2
    size = half * rows
    refs = list(refs)
    take = refs.pop
    got, spec, shift, inv, fwd, c_x, swap, mob, mob_lo, mob_hi = [take(0) for _ in range(10)]
    if not first_call:
        dir_old, q_old, rho_old = [take(0) for _ in range(3)]
    direction, image = take(0), take(0)
    if last_call:
        rho_out, part_out = take(0), take(0)
    else:
        rho_out, dir_spec, q_out, image_spec, message = [take(0) for _ in range(5)]
    work, q_mid, fold = take(0), take(0), take(0)
    if last_call:
        dir_spec, q_out = take(0), take(0)

    total = jnp.zeros((1, LANES), f32)
    for o in range(depth):
        q_mid[o : o + 1, :] = got[o, 0:1, :span]
        q_mid[depth + o : depth + o + 1, :] = got[o, 0:1, span : 2 * span]
        total = total + got[o, 0:1, 2 * span :]
    rho = jnp.sum(total, axis=1, keepdims=True) + jnp.zeros((1, LANES), f32)
    rho_out[...] = rho
    if not first_call:
        beta = (rho / rho_old[...])[:, :1]
    for parity in range(2):
        at_q = parity * half
        mu = shift[at_q : at_q + half, :]
        q_lo = q_mid[at_q : at_q + half, :]
        q_hi = q_mid[depth + at_q : depth + at_q + half, :]
        for ky in range(rows):
            at = parity * size + ky * half
            u = (spec[at : at + half, :] + tab["first"][ky] * q_lo - tab["last"][ky] * q_hi) / (
                mu + tab["lam"][ky]
            )
            if not first_call:
                u = u + beta * dir_old[at : at + half, :]
            dir_spec[at : at + half, :] = u
    q = q_mid[...]
    if not first_call:
        q = q + beta * q_old[...]
    q_out[...] = q
    q_mid[...] = mat(swap[...], mat(q, c_x[...]))
    for parity in range(2):
        fold[parity * size : (parity + 1) * size, :] = mat(
            inv[parity], mat(dir_spec[parity * size : (parity + 1) * size, :], c_x[...])
        )
    for z in range(half):
        a = fold[z * rows : (z + 1) * rows, :]
        b = fold[size + z * rows : size + (z + 1) * rows, :]
        direction[z * rows : (z + 1) * rows, :] = a + b
        direction[(depth - 1 - z) * rows : (depth - z) * rows, :] = a - b

    r = lax.broadcasted_iota(jnp.int32, (rows, span), 0)
    c = lax.broadcasted_iota(jnp.int32, (rows, span), 1)
    acc = jnp.zeros((1, span), f32)
    below = None
    for z in range(depth):
        at = slice(z * rows, (z + 1) * rows)
        v = direction[at, :]
        b = mob[at, :]
        out = compress * v
        flux = jnp.where(c == span - 1, 0.0, (b + lane_roll(b, True)) * (v - lane_roll(v, True)))
        out_flux = flux - lane_roll(flux, False)
        b_hi = b[rows - 1 :] + mob_hi[z : z + 1, :]
        flux = jnp.where(
            r == rows - 1,
            b_hi * q_mid[depth + z : depth + z + 1, :],
            (b + row_roll(b, True)) * (v - row_roll(v, True)),
        )
        f_lo = (b[:1] + mob_lo[z : z + 1, :]) * q_mid[z : z + 1, :]
        out_flux = out_flux + flux - jnp.where(r == 0, f_lo, row_roll(flux, False))
        if below is not None:
            out_flux = out_flux - below
        if z + 1 < depth:
            up = slice((z + 1) * rows, (z + 2) * rows)
            below = (b + mob[up, :]) * (v - direction[up, :])
            out_flux = out_flux + below
        out = out + 0.5 * out_flux
        image[at, :] = out
        acc = acc + jnp.sum(v * out, axis=0, keepdims=True)
    part = fold_lanes(acc)
    if last_call:
        for i in range(blocks):
            part_out[i] = part
    else:
        forward_body(dims, tab, image, work, image_spec, fwd, c_x, shift, message, part)


def on_device(superheat_excess, liquid_indicator, listing, smear_n, smear_e):
    thick, north, span = superheat_excess.shape
    wide, lanes = lax.axis_size("wide"), lax.axis_size("narrow")
    w, n = lax.axis_index("wide"), lax.axis_index("narrow")
    blocks = wide * lanes
    depth = thick * wide
    rows = north // wide
    size_y, size_x = smear_n.shape[0], smear_e.shape[0]
    tiles_y = north // size_y
    dims = (depth, rows, span)
    tab = tables(depth, rows, span, blocks)
    own = n * wide + w
    whole = depth * rows

    phase = liquid_indicator.astype(f32)
    both = jnp.stack([superheat_excess, phase])
    up = [(i, i + 1) for i in range(wide - 1)]
    down = [(i + 1, i) for i in range(wide - 1)]
    zlo = lax.ppermute(both[:, thick - 1], "wide", up)
    zhi = lax.ppermute(both[:, 0], "wide", down)
    up = [(i, i + 1) for i in range(lanes - 1)]
    down = [(i + 1, i) for i in range(lanes - 1)]
    ylo = lax.ppermute(both[:, :, north - 1 :], "narrow", up)
    yhi = lax.ppermute(both[:, :, :1], "narrow", down)

    def regroup(x):
        x = x.reshape(wide, thick * rows, span)
        return lax.all_to_all(x, "wide", split_axis=0, concat_axis=0, tiled=True)

    mob = jnp.where(phase > 0.5, mobility_liquid, mobility_vapor)
    mob = mob.reshape(thick, wide, rows, span).transpose(1, 0, 2, 3)
    mob = regroup(mob).reshape(depth, rows, span)

    def place(j):
        return (j % wide) * lanes + j // wide

    up = [(place(j), place(j + 1)) for j in range(blocks - 1)]
    down = [(b, a) for a, b in up]
    mob_lo = lax.ppermute(mob[:, rows - 1], ("wide", "narrow"), up)
    mob_hi = lax.ppermute(mob[:, 0], ("wide", "narrow"), down)
    mob = mob.reshape(whole, span)

    pos = jnp.stack([w, wide - 1 - w, n, lanes - 1 - n]).astype(jnp.int32)
    blockn = (jnp.eye(tiles_y, dtype=f32)[:, None, :, None] * smear_n[None, :, None, :]).reshape(
        north, north
    )
    most = listing.size
    heat_dims = (thick, north, span, size_y, size_x, most)
    heated, source = call(
        lambda *r: heat_body(heat_dims, *r),
        [(thick, north, span), (tiles_y, thick, size_y, span)],
        pos, listing.reshape(-1), superheat_excess, liquid_indicator, zlo, zhi, ylo, yhi, blockn, smear_e,
        smem=(0, 1),
        scratch=[
            VMEM((thick + 2, north, span), f32),
            VMEM((thick + 2, north, span), f32),
            VMEM((thick * north, span), f32),
            VMEM((tiles_y, span), f32),
        ],
        name="heat",
    )
    if size_y != rows:
        source = source.transpose(1, 0, 2, 3).reshape(thick, wide, rows, span).transpose(1, 0, 2, 3)
    source = regroup(source).reshape(whole, span)

    c_x, fwd, inv = (jnp.asarray(tab[k]) for k in ("c_x", "forward", "inverse"))
    swap, shift, sine, wave = (jnp.asarray(tab[k]) for k in ("swap", "shift", "sine", "wave"))
    pair = lax.dynamic_index_in_dim(jnp.asarray(tab["pair"]), own, 0, keepdims=False)
    full = (whole, span)
    letter = (blocks, 1, 2 * span + LANES)
    one = (1, LANES)

    def swap_all(x):
        return lax.all_to_all(x, ORDER, split_axis=0, concat_axis=0, tiled=True)

    spec, message = call(
        lambda *r: start_body(dims, tab, *r), [full, letter], source, fwd, c_x, shift,
        scratch=[VMEM(full, f32)], name="start",
    )
    pair_scratch = [VMEM((blocks, span), f32)] * 2
    jump, message = call(
        lambda *r: solve_body(dims, tab, True, blocks, *r), [(blocks, span), letter],
        swap_all(message), spec, shift, pair, sine, wave, scratch=pair_scratch, name="solve",
    )
    pressure, residual = None, source
    dir_spec = q = rho = None
    for iteration in range(ITERS):
        first, final = iteration == 0, iteration + 1 == ITERS
        args = [swap_all(message), spec, shift, inv, fwd, c_x, swap, mob, mob_lo, mob_hi]
        if not first:
            args += [dir_spec, q, rho]
        outs = [full, full, one]
        work = [VMEM(full, f32), VMEM((2 * depth, span), f32), VMEM(full, f32)]
        if final:
            outs += [(blocks, 1, LANES)]
            work += [VMEM(full, f32), VMEM((2 * depth, span), f32)]
        else:
            outs += [full, (2 * depth, span), full, letter]
        result = call(
            lambda *r, a=first, b=final: advance_body(dims, tab, a, b, blocks, *r), outs, *args,
            scratch=work, name="advance",
        )
        direction, image, rho = result[:3]
        if final:
            bottom = jnp.sum(swap_all(result[3]))
            alpha = rho[0, 0] / bottom
        else:
            dir_spec, q, image_spec, message = result[3:]
            spec, jump, message, alpha = call(
                lambda *r: solve_body(dims, tab, False, blocks, *r),
                [full, (blocks, span), letter, one],
                swap_all(message), spec, shift, pair, sine, wave, image_spec, jump, rho,
                scratch=pair_scratch, name="solve",
            )
            alpha = alpha[0, 0]
        pressure = alpha * direction if first else pressure + alpha * direction
        residual = residual - alpha * image

    both = jnp.stack([pressure, residual]).reshape(2, wide, thick, rows, span)
    both = lax.all_to_all(both, "wide", split_axis=1, concat_axis=1, tiled=True)
    both = both.transpose(0, 2, 1, 3, 4).reshape(2, thick, north, span)
    return heated, both[0], both[1]


def solution(mesh):
    spec = P("wide", "narrow", None)
    return jax.shard_map(
        on_device,
        mesh=mesh,
        in_specs=(spec, spec, spec, P(), P()),
        out_specs=(spec, spec, spec),
        check_vma=False,
    )
```

time: 663 us -> 277 us (0.42); the launches traced: 652 us -> 276 us
  blocking collectives: 356 us -> 138 us
  matrix products: 102 us -> 0 us
  waiting for transfers between devices: 85.3 us -> 50.1 us
  Pallas kernels: 0 us -> 33.5 us
  other arithmetic: 39 us -> 7.64 us
  starting transfers between devices: 42.4 us -> 26.7 us
  between operations: 8.73 us -> 1.74 us
    psum x5 -> x0, blocking collectives: 205 us -> none  [the longest x3 119 us: inner(): return lax.psum(jnp.sum(first_field * second_field), ('wide', 'narrow'))]
    dot_general x22 -> x0, matrix products: 102 us -> none  [the longest x3 31.3 us: precondition(): spectrum = jnp.einsum('zyx,kx->zyk', remainder, table_x, precision=highest)]
    ppermute x16 -> x6, waiting for transfers between devices: 59.4 us -> 20.9 us  [the longest x1 10.6 us: on_device(): zlo = lax.ppermute(both[:, thick - 1], 'wide', up)]
    pallas_call x0 -> x8, Pallas kernels: none -> 33.5 us  [call(): pl.pallas_call(body, out_shape=[jax.ShapeDtypeStruct(s, f32) for s in out...]
    ppermute x16 -> x6, starting transfers between devices: 34.4 us -> 16.4 us  [the longest x1 5.56 us: on_device(): zlo = lax.ppermute(both[:, thick - 1], 'wide', up)]
    all_to_all x5 -> x7, blocking collectives: 151 us -> 138 us  [the longest x5 55.2 us: swap_all(): return lax.all_to_all(x, ORDER, split_axis=0, concat_axis=0, tiled=True)]
    reduce_sum x3 -> x1, other arithmetic: 12.9 us -> 0.72 us  [on_device(): bottom = jnp.sum(swap_all(result[3]))]
    unnamed x53 -> x64, local copies, waits for them, and re-layouts: 4.71 us -> 14.7 us
  transfers between devices with their start and end apart: 17 -> 9, of which waited for: 9 -> 7; matrix products, arithmetic and copies ran while one was open for 0% -> 1% of each run, Pallas kernels for 0% -> 0%
where the time goes in v1:
time: 277 us; the launch traced here: 276 us
  blocking collectives  138 us (50%)
  waiting for transfers between devices  50.1 us (18%)
  Pallas kernels  33.5 us (12%)
  starting transfers between devices  26.7 us (10%)
  local copies, waits for them, and re-layouts  18.6 us (7%)
  other arithmetic  7.64 us (3%)
    all_to_all x5, blocking collectives, swap_all(): return lax.all_to_all(x, ORDER, split_axis=0, concat_axis=0, tiled=True)  55.2 us
    all_to_all x1, blocking collectives, on_device(): both = lax.all_to_all(both, 'wide', split_axis=1, concat_axis=1, tiled=True)  50.9 us
    pallas_call x8, Pallas kernels, call(): pl.pallas_call(body, out_shape=[jax.ShapeDtypeStruct(s, f32) for s in out...  33.5 us
    all_to_all x1, blocking collectives, regroup(): return lax.all_to_all(x, 'wide', split_axis=0, concat_axis=0, tiled=True)  31.5 us
    all_to_all x1, waiting for transfers between devices, regroup(): return lax.all_to_all(x, 'wide', split_axis=0, concat_axis=0, tiled=True)  22.5 us
    unnamed x64, local copies, waits for them, and re-layouts  14.7 us
    ppermute x1, waiting for transfers between devices, on_device(): zlo = lax.ppermute(both[:, thick - 1], 'wide', up)  10.6 us
    all_to_all x2, starting transfers between devices, swap_all(): return lax.all_to_all(x, ORDER, split_axis=0, concat_axis=0, tiled=True)  6.7 us
  transfers between devices with their start and end apart: 9, of which 7 were waited for; matrix products, arithmetic and copies ran while one was open for 1% of the time, Pallas kernels for 0%

profile of v1, /device:TPU:0, one launch (start us, length us, event | category | flops | bytes accessed | tf_op | source)
XLA Modules:
  0.0 275.8 jit_solution(5820691397621394816)
XLA Ops:
  0.6 1.4 convert_bitcast_fusion
  3.0 1.4 collective-permute-start.1
  4.5 5.6 %collective-permute-start = (f32[2,128,512]{2,1,0:T(8,128)S(1)}, f32[2,128,512]{2,1,0:T(8,128)S(1)}, u32[]{:S(2)}, u32[]{:S(2)}) collective-permute-start(f32[2,128,512]{2,1,0:T(8,128)S(1)} %get-tuple-element.70), channel_id=1, source_target_pairs={{0,4},{4,8},{8,12},{12,16},{16,20},{20,24},{24,28},{1,5},{5,9},{9,... | collective-permute-start | bytes 1572872 | tf_op jit(solution)/shard_map/ppermute | solution.py:400
  10.1 1.3 collective-permute-start.3
  11.4 3.0 %collective-permute-start.2 = (f32[2,4,1,512]{3,2,1,0:T(1,128)S(1)}, f32[2,4,1,512]{3,2,1,0:T(1,128)S(1)}, u32[]{:S(2)}, u32[]{:S(2)}) collective-permute-start(f32[2,4,1,512]{3,2,1,0:T(1,128)S(1)} %get-tuple-element.68), channel_id=1, source_target_pairs={{0,1},{1,2},{2,3},{4,5},{5,6},{6,7},{8,9},{9,10},{10,11},{12,13},{... | collective-permute-start | bytes 49160 | tf_op jit(solution)/shard_map/ppermute | solution.py:404
  15.2 5.0 %collective-permute-done.1.r_5_ = f32[2,128,512]{2,1,0:T(8,128)S(1)} collective-permute-done((f32[2,128,512]{2,1,0:T(8,128)}, f32[2,128,512]{2,1,0:T(8,128)S(1)}, u32[]{:S(2)}, u32[]{:S(2)}) %collective-permute-start.1) | collective-permute-done | bytes 524320 | tf_op jit(solution)/shard_map/ppermute | solution.py:401
  21.0 10.6 %collective-permute-done.r_4_ = f32[2,128,512]{2,1,0:T(8,128)S(1)} collective-permute-done((f32[2,128,512]{2,1,0:T(8,128)S(1)}, f32[2,128,512]{2,1,0:T(8,128)S(1)}, u32[]{:S(2)}, u32[]{:S(2)}) %collective-permute-start) | collective-permute-done | bytes 524320 | tf_op jit(solution)/shard_map/ppermute | solution.py:400
  32.4 1.2 copy-done.5
  35.7 5.0 %heat.1 = (f32[4,128,512]{2,1,0:T(8,128)}, f32[8,4,16,512]{3,2,1,0:T(8,128)S(1)}) custom-call(s32[4]{0:T(128)S(1)} %pad_add_fusion.r_0_, s32[16]{0:T(128)S(1)} %bitcast.58, f32[4,128,512]{2,1,0:T(8,128)S(1)} %copy-done.3, s32[4,128,512]{2,1,0:T(8,128)S(1)} %copy-done.5, f32[2,128,512]{2,1,0:T(8,128)S(1)} %copy-done.22, f32[2,128,512]{2,1,0:T(8,128)S(1)} %copy-done.20, ...), custom_call_target="tpu_custom_call" | custom-call | flops 1000000000 | bytes 4194304 | tf_op jit(solution)/shard_map/heat/pallas_call | solution.py:96
  40.7 31.5 %all_to_all.50 = f32[8,64,512]{2,1,0:T(8,128)S(1)} all-to-all(f32[8,64,512]{2,1,0:T(8,128)S(1)} %bitcast.55), channel_id=1, replica_groups=mesh['wide'=8,'narrow'=4] {'wide'}, dimensions={0} | all-to-all | bytes 2097152 | tf_op jit(solution)/shard_map/all_to_all | solution.py:409
  72.2 3.8 %start.1 = (f32[512,512]{1,0:T(8,128)S(1)}, f32[32,1,1152]{2,1,0:T(1,128)}) custom-call(f32[512,512]{1,0:T(8,128)S(1)} %bitcast.54, f32[2,256,256]{2,1,0:T(8,128)S(1)} %copy-done.1, f32[512,512]{1,0:T(8,128)S(1)} %copy-done, f32[32,512]{1,0:T(8,128)S(1)} %copy-done.16), custom_call_target="tpu_custom_call" | custom-call | flops 1000000000 | bytes 4194304 | tf_op jit(solution)/shard_map/start/pallas_call | solution.py:96
  77.9 3.7 %all-to-all-start.1 = ((f32[32,1,1152]{2,1,0:T(1,128)}), f32[32,1,1152]{2,1,0:T(1,128)S(1)}, u32[]{:S(2)}, u32[]{:S(2)}) async-start(f32[32,1,1152]{2,1,0:T(1,128)} %get-tuple-element.36), calls=%async_computation.1 | async-start | bytes 294912 | tf_op jit(solution)/shard_map/all_to_all | solution.py:455
  82.8 6.6 %all-to-all-done.1.r_0_ = f32[32,1,1152]{2,1,0:T(1,128)S(1)} async-done(((f32[32,1,1152]{2,1,0:T(1,128)}), f32[32,1,1152]{2,1,0:T(1,128)S(1)}, u32[]{:S(2)}, u32[]{:S(2)}) %all-to-all-start.1) | async-done | bytes 147488 | tf_op jit(solution)/shard_map/all_to_all | solution.py:455
  89.5 3.6 %all-to-all-start.3 = ((f32[8,64,512]{2,1,0:T(8,128)}), f32[8,64,512]{2,1,0:T(8,128)S(1)}, u32[]{:S(2)}, u32[]{:S(2)}) async-start(f32[8,64,512]{2,1,0:T(8,128)} %bitcast.61), calls=%async_computation.3 | async-start | bytes 2097152 | tf_op jit(solution)/shard_map/all_to_all | solution.py:409
  93.7 1.2 copy-done.14
  96.8 22.5 %all-to-all-done.3 = f32[8,64,512]{2,1,0:T(8,128)S(1)} async-done(((f32[8,64,512]{2,1,0:T(8,128)}), f32[8,64,512]{2,1,0:T(8,128)S(1)}, u32[]{:S(2)}, u32[]{:S(2)}) %all-to-all-start.3) | async-done | bytes 1048608 | tf_op jit(solution)/shard_map/all_to_all | solution.py:409
  119.3 3.0 %all-to-all-start.2 = ((f32[32,1,1152]{2,1,0:T(1,128)}), f32[32,1,1152]{2,1,0:T(1,128)S(1)}, u32[]{:S(2)}, u32[]{:S(2)}) async-start(f32[32,1,1152]{2,1,0:T(1,128)} %copy-done.18), calls=%async_computation.2 | async-start | bytes 294912 | tf_op jit(solution)/shard_map/all_to_all | solution.py:455
  122.5 3.7 %collective-permute-start.4 = (f32[32,512]{1,0:T(8,128)S(1)}, f32[32,512]{1,0:T(8,128)S(1)}, u32[]{:S(2)}, u32[]{:S(2)}) collective-permute-start(f32[32,512]{1,0:T(8,128)S(1)} %bitcast.68), channel_id=1, source_target_pairs={{0,4},{4,8},{8,12},{12,16},{16,20},{20,24},{24,28},{28,1},{1,5},{5... | collective-permute-start | bytes 196616 | tf_op jit(solution)/shard_map/ppermute | solution.py:420
  126.2 1.5 collective-permute-start.5
  128.1 4.5 %collective-permute-done.5.r_9_ = f32[32,512]{1,0:T(8,128)S(1)} collective-permute-done((f32[32,512]{1,0:T(8,128)S(1)}, f32[32,512]{1,0:T(8,128)S(1)}, u32[]{:S(2)}, u32[]{:S(2)}) %collective-permute-start.5) | collective-permute-done | bytes 65568 | tf_op jit(solution)/shard_map/ppermute | solution.py:421
  132.6 1.2 copy-done.15
  133.8 8.5 %advance.3 = (f32[512,512]{1,0:T(8,128)S(1)}, f32[512,512]{1,0:T(8,128)S(1)}, f32[1,128]{1,0:T(1,128)S(1)}, f32[512,512]{1,0:T(8,128)S(1)}, f32[64,512]{1,0:T(8,...) custom-call(f32[32,1,1152]{2,1,0:T(1,128)S(1)} %all-to-all-done.2.r_0_, f32[512,512]{1,0:T(8,128)S(1)} %copy-done.15, ...), custom_call_target="tpu_custom_call" | custom-call | flops 1000000000 | bytes 4194304 | tf_op jit(solution)/shard_map/advance/pallas_call | solution.py:96
  143.3 14.7 %all_to_all.51.r_0_ = f32[32,1,1152]{2,1,0:T(1,128)S(1)} all-to-all(f32[32,1,1152]{2,1,0:T(1,128)S(1)} %get-tuple-element.39), channel_id=1, replica_groups=mesh['wide'=8,'narrow'=4] {'narrow','wide'}, dimensions={0} | all-to-all | bytes 294912 | tf_op jit(solution)/shard_map/all_to_all | solution.py:455
  158.6 10.3 %all_to_all.52.r_0_ = f32[32,1,1152]{2,1,0:T(1,128)S(1)} all-to-all(f32[32,1,1152]{2,1,0:T(1,128)S(1)} %get-tuple-element.45), channel_id=1, replica_groups=mesh['wide'=8,'narrow'=4] {'narrow','wide'}, dimensions={0} | all-to-all | bytes 294912 | tf_op jit(solution)/shard_map/all_to_all | solution.py:455
  168.9 8.5 %advance.4 = (f32[512,512]{1,0:T(8,128)S(1)}, f32[512,512]{1,0:T(8,128)S(1)}, f32[1,128]{1,0:T(1,128)S(1)}, f32[512,512]{1,0:T(8,128)S(1)}, f32[64,512]{1,0:T(8,...) custom-call(f32[32,1,1152]{2,1,0:T(1,128)S(1)} %all_to_all.52.r_0_, f32[512,512]{1,0:T(8,128)S(1)} %get-tuple-element.46.r_1_, ...), custom_call_target="tpu_custom_call" | custom-call | flops 1000000000 | bytes 4194304 | tf_op jit(solution)/shard_map/advance/pallas_call | solution.py:96
  178.4 10.3 %all_to_all.53.r_0_ = f32[32,1,1152]{2,1,0:T(1,128)S(1)} all-to-all(f32[32,1,1152]{2,1,0:T(1,128)S(1)} %get-tuple-element.49), channel_id=1, replica_groups=mesh['wide'=8,'narrow'=4] {'narrow','wide'}, dimensions={0} | all-to-all | bytes 294912 | tf_op jit(solution)/shard_map/all_to_all | solution.py:455
  189.8 10.3 %all_to_all.54.r_0_ = f32[32,1,1152]{2,1,0:T(1,128)S(1)} all-to-all(f32[32,1,1152]{2,1,0:T(1,128)S(1)} %get-tuple-element.55), channel_id=1, replica_groups=mesh['wide'=8,'narrow'=4] {'narrow','wide'}, dimensions={0} | all-to-all | bytes 294912 | tf_op jit(solution)/shard_map/all_to_all | solution.py:455
  200.1 5.5 %advance.5 = (f32[512,512]{1,0:T(8,128)S(1)}, f32[512,512]{1,0:T(8,128)S(1)}, f32[1,128]{1,0:T(1,128)S(1)}, f32[32,1,128]{2,1,0:T(1,128)S(1)}) custom-call(f32[32,1,1152]{2,1,0:T(1,128)S(1)} %all_to_all.54.r_0_, f32[512,512]{1,0:T(8,128)S(1)} %get-tuple-element.56.r_1_, f32[32,512]{1,0:T(8,128)S(1)} %copy-done.16, f32[2,256,256]{2,1,0:T(8,128)S(1)} %copy-done.2, ...), custom_call_target="tpu_custom_call" | custom-call | flops 1000000000 | bytes 4194304 | tf_op jit(solution)/shard_map/advance/pallas_call | solution.py:96
  207.6 9.6 %all_to_all.55 = f32[32,1,128]{2,1,0:T(1,128)S(1)} all-to-all(f32[32,1,128]{2,1,0:T(1,128)S(1)} %get-tuple-element.60), channel_id=1, replica_groups=mesh['wide'=8,'narrow'=4] {'narrow','wide'}, dimensions={0} | all-to-all | bytes 32768 | tf_op jit(solution)/shard_map/all_to_all | solution.py:455
  218.7 4.0 %multiply_subtract_fusion = (f32[512,512]{1,0:T(8,128)S(1)}, f32[512,512]{1,0:T(8,128)S(1)}) fusion(f32[512,512]{1,0:T(8,128)} %copy-done.12, f32[512,512]{1,0:T(8,128)} %copy-done.10, f32[512,512]{1,0:T(8,128)} %copy-done.8, f32[]{:T(128)S(6)} %div.3, f32[]{:T(128)S(1)} %bitcast.57, f32[]{:T(128)S(1)} %bitcast.56, f32[8,64,512]{2,1,0:T(8,128)} %copy-done.4, ...), kind=kLoop, calls=%fused_computation.8 | loop fusion | flops 2883584 | bytes 9437196 | tf_op jit(solution)/shard_map/sub | solution.py:498
  223.0 50.9 %all_to_all.56 = f32[2,8,4,16,512]{4,3,2,0,1:T(8,128)S(1)} all-to-all(f32[2,8,4,16,512]{4,3,2,0,1:T(8,128)S(1)} %pad_maximum_fusion), channel_id=1, replica_groups=mesh['wide'=8,'narrow'=4] {'wide'}, dimensions={1} | all-to-all | bytes 4194304 | tf_op jit(solution)/shard_map/all_to_all | solution.py:501
  274.2 1.6 fusion.7
  (81 shorter events, 18.7 us)
Async XLA Ops:
  0.6 1.5 copy-start.3
  2.2 12.2 %copy-start.30 = (f32[16,16]{1,0:T(8,128)S(1)}, f32[16,16]{1,0:T(8,128)}, u32[]{:S(2)}) copy-start(f32[16,16]{1,0:T(8,128)} %param.16) | copy-start | bytes 3076
  3.0 29.3 %copy-start.23 = (f32[128,128]{1,0:T(8,128)S(1)}, f32[128,128]{1,0:T(8,128)}, u32[]{:S(2)}) copy-start(f32[128,128]{1,0:T(8,128)} %r_9_.1) | copy-start | bytes 196612
  3.0 29.3 %copy-start.24 = (s32[1,1,16]{2,1,0:T(1,128)S(1)}, s32[1,1,16]{2,1,0:T(1,128)}, u32[]{:S(2)}) copy-start(s32[1,1,16]{2,1,0:T(1,128)} %param.15) | copy-start | bytes 196
  3.0 17.1 %collective-permute-start.1 = (f32[2,128,512]{2,1,0:T(8,128)}, f32[2,128,512]{2,1,0:T(8,128)S(1)}, u32[]{:S(2)}, u32[]{:S(2)}) collective-permute-start(f32[2,128,512]{2,1,0:T(8,128)} %get-tuple-element.69), channel_id=1, source_target_pairs={{4,0},{8,4},{12,8},{16,12},{20,16},{24,20},{28,24},{5,1},{9,5},{13... | collective-permute-start | bytes 1572872 | tf_op jit(solution)/shard_map/ppermute | solution.py:401
  4.5 27.1 %collective-permute-start = (f32[2,128,512]{2,1,0:T(8,128)S(1)}, f32[2,128,512]{2,1,0:T(8,128)S(1)}, u32[]{:S(2)}, u32[]{:S(2)}) collective-permute-start(f32[2,128,512]{2,1,0:T(8,128)S(1)} %get-tuple-element.70), channel_id=1, source_target_pairs={{0,4},{4,8},{8,12},{12,16},{16,20},{20,24},{24,28},{1,5},{5,9},{9,... | collective-permute-start | bytes 1572872 | tf_op jit(solution)/shard_map/ppermute | solution.py:400
  10.1 4.8 %collective-permute-start.3 = (f32[2,4,1,512]{3,2,1,0:T(1,128)S(1)}, f32[2,4,1,512]{3,2,1,0:T(1,128)S(1)}, u32[]{:S(2)}, u32[]{:S(2)}) collective-permute-start(f32[2,4,1,512]{3,2,1,0:T(1,128)S(1)} %get-tuple-element.67), channel_id=1, source_target_pairs={{1,0},{2,1},{3,2},{5,4},{6,5},{7,6},{9,8},{10,9},{11,10},{13,12},{... | collective-permute-start | bytes 49160 | tf_op jit(solution)/shard_map/ppermute | solution.py:405
  11.4 3.9 %collective-permute-start.2 = (f32[2,4,1,512]{3,2,1,0:T(1,128)S(1)}, f32[2,4,1,512]{3,2,1,0:T(1,128)S(1)}, u32[]{:S(2)}, u32[]{:S(2)}) collective-permute-start(f32[2,4,1,512]{3,2,1,0:T(1,128)S(1)} %get-tuple-element.68), channel_id=1, source_target_pairs={{0,1},{1,2},{2,3},{4,5},{5,6},{6,7},{8,9},{9,10},{10,11},{12,13},{... | collective-permute-start | bytes 49160 | tf_op jit(solution)/shard_map/ppermute | solution.py:404
  32.4 1.2 copy-start.5
  33.6 1.0 copy-start.20
  34.6 1.0 copy-start.22
  35.7 36.5 %copy-start = (f32[512,512]{1,0:T(8,128)S(1)}, f32[512,512]{1,0:T(8,128)}, u32[]{:S(2)}) copy-start(f32[512,512]{1,0:T(8,128)} %constant.45.clone.r_2_.r_5_) | copy-start | bytes 3145732
  35.7 36.5 %copy-start.1 = (f32[2,256,256]{2,1,0:T(8,128)S(1)}, f32[2,256,256]{2,1,0:T(8,128)}, u32[]{:S(2)}) copy-start(f32[2,256,256]{2,1,0:T(8,128)} %constant.46.clone.r_1_.r_4_) | copy-start | bytes 1572868
  35.7 36.5 %copy-start.16 = (f32[32,512]{1,0:T(8,128)S(1)}, f32[32,512]{1,0:T(8,128)}, u32[]{:S(2)}) copy-start(f32[32,512]{1,0:T(8,128)} %constant.49.clone.r_3_.r_2_) | copy-start | bytes 196612
  72.2 9.4 %copy-start.6 = (s32[4,128,512]{2,1,0:T(8,128)S(1)}, s32[4,128,512]{2,1,0:T(8,128)}, u32[]{:S(2)}) copy-start(s32[4,128,512]{2,1,0:T(8,128)} %r_3_.5) | copy-start | bytes 3145732
  75.9 1.0 copy-start.4
  77.9 11.6 %all-to-all-start.1 = ((f32[32,1,1152]{2,1,0:T(1,128)}), f32[32,1,1152]{2,1,0:T(1,128)S(1)}, u32[]{:S(2)}, u32[]{:S(2)}) async-start(f32[32,1,1152]{2,1,0:T(1,128)} %get-tuple-element.36), calls=%async_computation.1 | async-start | bytes 294912 | tf_op jit(solution)/shard_map/all_to_all | solution.py:455
  81.7 12.0 %copy-start.25 = (f32[32,128]{1,0:T(8,128)S(1)}, f32[32,128]{1,0:T(8,128)}, u32[]{:S(2)}) copy-start(f32[32,128]{1,0:T(8,128)} %constant.51.clone.r_5_) | copy-start | bytes 49156
  81.7 12.0 %copy-start.26 = (f32[32,32]{1,0:T(8,128)S(1)}, f32[32,32]{1,0:T(8,128)}, u32[]{:S(2)}) copy-start(f32[32,32]{1,0:T(8,128)} %constant.50.clone.r_4_) | copy-start | bytes 12292
  89.5 29.8 %all-to-all-start.3 = ((f32[8,64,512]{2,1,0:T(8,128)}), f32[8,64,512]{2,1,0:T(8,128)S(1)}, u32[]{:S(2)}, u32[]{:S(2)}) async-start(f32[8,64,512]{2,1,0:T(8,128)} %bitcast.61), calls=%async_computation.3 | async-start | bytes 2097152 | tf_op jit(solution)/shard_map/all_to_all | solution.py:409
  93.7 1.2 copy-start.14
  95.0 37.7 %copy-start.2 = (f32[2,256,256]{2,1,0:T(8,128)S(1)}, f32[2,256,256]{2,1,0:T(8,128)}, u32[]{:S(2)}) copy-start(f32[2,256,256]{2,1,0:T(8,128)} %constant.47.clone.r_3_) | copy-start | bytes 1572868
  95.0 37.7 %copy-start.17 = (f32[64,64]{1,0:T(8,128)S(1)}, f32[64,64]{1,0:T(8,128)}, u32[]{:S(2)}) copy-start(f32[64,64]{1,0:T(8,128)} %constant.48.clone.r_6_) | copy-start | bytes 49156
  119.3 13.3 %all-to-all-start.2 = ((f32[32,1,1152]{2,1,0:T(1,128)}), f32[32,1,1152]{2,1,0:T(1,128)S(1)}, u32[]{:S(2)}, u32[]{:S(2)}) async-start(f32[32,1,1152]{2,1,0:T(1,128)} %copy-done.18), calls=%async_computation.2 | async-start | bytes 294912 | tf_op jit(solution)/shard_map/all_to_all | solution.py:455
  122.5 5.7 %collective-permute-start.4 = (f32[32,512]{1,0:T(8,128)S(1)}, f32[32,512]{1,0:T(8,128)S(1)}, u32[]{:S(2)}, u32[]{:S(2)}) collective-permute-start(f32[32,512]{1,0:T(8,128)S(1)} %bitcast.68), channel_id=1, source_target_pairs={{0,4},{4,8},{8,12},{12,16},{16,20},{20,24},{24,28},{28,1},{1,5},{5... | collective-permute-start | bytes 196616 | tf_op jit(solution)/shard_map/ppermute | solution.py:420
  126.2 6.4 %collective-permute-start.5 = (f32[32,512]{1,0:T(8,128)S(1)}, f32[32,512]{1,0:T(8,128)S(1)}, u32[]{:S(2)}, u32[]{:S(2)}) collective-permute-start(f32[32,512]{1,0:T(8,128)S(1)} %bitcast.67), channel_id=1, source_target_pairs={{4,0},{8,4},{12,8},{16,12},{20,16},{24,20},{28,24},{1,28},{5,1},{9... | collective-permute-start | bytes 196616 | tf_op jit(solution)/shard_map/ppermute | solution.py:421
  132.6 1.2 copy-start.15
  133.8 24.1 %copy-start.27 = (f32[32,32]{1,0:T(8,128)S(1)}, f32[32,32]{1,0:T(8,128)}, u32[]{:S(2)}) copy-start(f32[32,32]{1,0:T(8,128)} %constant.50.clone.r_4_) | copy-start | bytes 12292
  133.8 24.1 %copy-start.29 = (f32[32,512]{1,0:T(8,128)S(1)}, f32[32,512]{1,0:T(8,128)}, u32[]{:S(2)}) copy-start(f32[32,512]{1,0:T(8,128)} %copy-done.28) | copy-start | bytes 196612
  143.3 25.6 %copy-start.7 = (f32[512,512]{1,0:T(8,128)}, f32[512,512]{1,0:T(8,128)S(1)}, u32[]{:S(2)}) copy-start(f32[512,512]{1,0:T(8,128)S(1)} %get-tuple-element.44) | copy-start | bytes 3145732
  178.4 21.7 %copy-start.9 = (f32[512,512]{1,0:T(8,128)}, f32[512,512]{1,0:T(8,128)S(1)}, u32[]{:S(2)}) copy-start(f32[512,512]{1,0:T(8,128)S(1)} %get-tuple-element.54) | copy-start | bytes 3145732
  205.7 1.0 copy-start.11
  (8 other events, 6.8 us)

commit v2 on v1

--- a/solution.py
+++ b/solution.py
@@ -89,9 +89,10 @@
     }
 
 
-def call(body, outs, *args, smem=(), scratch=(), flops=1e9, name=None):
+def call(body, outs, *args, smem=(), far=(), scratch=(), flops=1e9, name=None):
     specs = [
-        pl.BlockSpec(memory_space=pltpu.SMEM if i in smem else VMEM) for i in range(len(args))
+        pl.BlockSpec(memory_space=pltpu.SMEM if i in smem else pl.ANY if i in far else VMEM)
+        for i in range(len(args))
     ]
     return pl.pallas_call(
         body,
@@ -99,7 +100,7 @@
         in_specs=specs,
         out_specs=[pl.BlockSpec(memory_space=VMEM)] * len(outs),
         scratch_shapes=list(scratch),
-        compiler_params=pltpu.CompilerParams(vmem_limit_bytes=40 * 2**20),
+        compiler_params=pltpu.CompilerParams(vmem_limit_bytes=16 * 2**20),
         cost_estimate=pl.CostEstimate(flops=int(flops), bytes_accessed=4 << 20, transcendentals=0),
         name=name,
     )(*args)
@@ -134,45 +135,80 @@
     return jnp.sum(total, axis=0, keepdims=True)
 
 
+def smear_blocks(smear, size):
+    n = smear.shape[0]
+    i = lax.broadcasted_iota(jnp.int32, (n, size), 0)
+    j = lax.broadcasted_iota(jnp.int32, (n, size), 1)
+    wide_pick = jnp.where(i == j % n, 1.0, 0.0)
+    i = lax.broadcasted_iota(jnp.int32, (size, n), 0)
+    j = lax.broadcasted_iota(jnp.int32, (size, n), 1)
+    tall_pick = jnp.where(i % n == j, 1.0, 0.0)
+    tiled = mat(tall_pick, mat(smear, wide_pick))
+    i = lax.broadcasted_iota(jnp.int32, (size, size), 0)
+    j = lax.broadcasted_iota(jnp.int32, (size, size), 1)
+    return jnp.where(i // n == j // n, tiled, 0.0)
+
+
+def conducted(t, p, pairs):
+    flux = jnp.zeros_like(t)
+    faces = jnp.zeros_like(t)
+    for near_t, near_p in pairs:
+        differ = near_p != p
+        flux = flux + jnp.where(differ, -2.0 * t, near_t - t)
+        faces = faces + jnp.where(differ, 1.0, 0.0)
+    k = jnp.where(p > 0.5, conduct_liquid, conduct_vapor)
+    value = t + diffusion * k * flux
+    return value, 2.0 * k * faces * value
+
+
 def heat_body(dims, *refs):
     thick, north, span, size_y, size_x, most = dims
-    (pos, table, temp, phase, zlo, zhi, ylo, yhi, smear_n, smear_e,
-     heated, source, tp, pp, mass, mask) = refs
+    with_source = most > 0
+    if with_source:
+        (table, temp, phase, zlo, zhi, ylo, yhi, smear, smear_e,
+         heated, source, tp, pp, mass, mask) = refs
+    else:
+        temp, phase, ylo, yhi, heated, pp = refs
+        tp = temp
+    base = 1 if with_source else 0
     tiles_y = north // size_y
     tiles_x = span // size_x
-    w_first, w_last = pos[0] == 0, pos[1] == 0
-    n_first, n_last = pos[2] == 0, pos[3] == 0
+    w, n = lax.axis_index("wide"), lax.axis_index("narrow")
+    n_first, n_last = n == 0, n == lax.axis_size("narrow") - 1
     for z in range(thick):
-        tp[z + 1] = temp[z]
-        pp[z + 1] = phase[z].astype(f32)
-    tp[0] = jnp.where(w_first, temp[0], zlo[0])
-    pp[0] = jnp.where(w_first, phase[0].astype(f32), zlo[1])
-    tp[thick + 1] = jnp.where(w_last, temp[thick - 1], zhi[0])
-    pp[thick + 1] = jnp.where(w_last, phase[thick - 1].astype(f32), zhi[1])
-    row = lax.broadcasted_iota(jnp.int32, (tiles_y, span), 0)
-    lane = lax.broadcasted_iota(jnp.int32, (tiles_y, span), 1)
-    tile = row * tiles_x + lane // size_x
-    hit = tile == table[0]
-    for i in range(1, most):
-        hit = jnp.logical_or(hit, tile == table[i])
-    mask[...] = jnp.where(hit, expansion, 0.0)
+        pp[z + base] = phase[z].astype(f32)
+    if with_source:
+        w_first, w_last = w == 0, w == lax.axis_size("wide") - 1
+        for z in range(thick):
+            tp[z + 1] = temp[z]
+        tp[0] = jnp.where(w_first, temp[0], zlo[0])
+        pp[0] = jnp.where(w_first, phase[0].astype(f32), zlo[1])
+        tp[thick + 1] = jnp.where(w_last, temp[thick - 1], zhi[0])
+        pp[thick + 1] = jnp.where(w_last, phase[thick - 1].astype(f32), zhi[1])
+        row = lax.broadcasted_iota(jnp.int32, (tiles_y, span), 0)
+        lane = lax.broadcasted_iota(jnp.int32, (tiles_y, span), 1)
+        tile = row * tiles_x + lane // size_x
+        hit = tile == table[0]
+        for i in range(1, most):
+            hit = jnp.logical_or(hit, tile == table[i])
+        mask[...] = jnp.where(hit, expansion, 0.0)
     r = lax.broadcasted_iota(jnp.int32, (size_y, span), 0)
     c = lax.broadcasted_iota(jnp.int32, (size_y, span), 1)
 
     def plane(z):
         for yc in range(tiles_y):
             at = pl.ds(yc * size_y, size_y)
-            t = tp[z + 1, at, :]
-            p = pp[z + 1, at, :]
+            t = tp[z + base, at, :]
+            p = pp[z + base, at, :]
 
             def edge(ref, halo, k, y, wall, own):
                 if 0 <= y < north:
-                    return ref[z + 1, pl.ds(y, 1), :]
+                    return ref[z + base, pl.ds(y, 1), :]
                 return jnp.where(wall, own, halo[k, z])
 
             pairs = [
-                (tp[z, at, :], pp[z, at, :]),
-                (tp[z + 2, at, :], pp[z + 2, at, :]),
+                (tp[z + base - 1, at, :], pp[z + base - 1, at, :]),
+                (tp[z + base + 1, at, :], pp[z + base + 1, at, :]),
                 (jnp.where(c == span - 1, t, lane_roll(t, True)),
                  jnp.where(c == span - 1, p, lane_roll(p, True))),
                 (jnp.where(c == 0, t, lane_roll(t, False)),
@@ -188,25 +224,174 @@
                 jnp.where(r == 0, edge(tp, ylo, 0, y, n_first, t[:1]), row_roll(t, False)),
                 jnp.where(r == 0, edge(pp, ylo, 1, y, n_first, p[:1]), row_roll(p, False)),
             ))
-            flux = jnp.zeros_like(t)
-            faces = jnp.zeros_like(t)
-            for near_t, near_p in pairs:
-                differ = near_p != p
-                flux = flux + jnp.where(differ, -2.0 * t, near_t - t)
-                faces = faces + jnp.where(differ, 1.0, 0.0)
-            k = jnp.where(p > 0.5, conduct_liquid, conduct_vapor)
-            value = t + diffusion * k * flux
-            heated[z, at, :] = value
-            mass[pl.ds(pl.multiple_of(z * north, north) + yc * size_y, size_y), :] = 2.0 * k * faces * value
-
-    lax.fori_loop(0, thick, lambda z, carry: (plane(z), carry)[1], 0)
+            value, vapor = conducted(t, p, pairs)
+            heated[z if with_source else z - 1, at, :] = value
+            if with_source:
+                to = pl.ds(pl.multiple_of(z * north, north) + yc * size_y, size_y)
+                mass[to, :] = vapor
+
+    inner = 1 - base
+    lax.fori_loop(inner, thick - inner, lambda z, carry: (plane(z), carry)[1], 0)
+    if not with_source:
+        return
+    smear_n = smear_blocks(smear[...], north)
     for tx in range(tiles_x):
         at = slice(tx * size_x, (tx + 1) * size_x)
         mass[:, at] = mat_t(mass[:, at], smear_e[...])
     for z in range(thick):
-        smeared = mat(smear_n[...], mass[z * north : (z + 1) * north, :])
+        smeared = mat(smear_n, mass[z * north : (z + 1) * north, :])
         for yc in range(tiles_y):
             source[yc, z] = smeared[yc * size_y : (yc + 1) * size_y] * mask[yc : yc + 1, :]
+
+
+def pack_body(dims, listing, far_temp, far_phase, out, side_first, side_last, temp, phase, entry, sems):
+    wide, thick, rows, span, most = dims
+    tiles = span // LANES
+    per = thick * tiles * rows
+    north = wide * rows
+    copies = [
+        pltpu.make_async_copy(far_temp, temp, sems.at[0]),
+        pltpu.make_async_copy(far_phase, phase, sems.at[1]),
+    ]
+    for copy in copies:
+        copy.start()
+    entry[...] = jnp.full((8, LANES), -1.0, f32)
+    entry[0:1, 0:most] = listing[0].astype(f32)
+    for w in range(wide):
+        out[w, 2 * per :, :] = entry[...]
+    for a, ref in enumerate((temp, phase)):
+        copies[a].wait()
+        for z in range(thick):
+            side_first[a, z] = ref[z, 0:1, :].astype(f32)
+            side_last[a, z] = ref[z, north - 1 : north, :].astype(f32)
+            for w in range(wide):
+                for t in range(tiles):
+                    at = a * per + (z * tiles + t) * rows
+                    piece = ref[z, w * rows : (w + 1) * rows, t * LANES : (t + 1) * LANES]
+                    out[w, at : at + rows, :] = piece.astype(f32)
+
+
+def edge_body(dims, got, first, last):
+    wide, thick, rows, span, _ = dims
+    tiles = span // LANES
+    per = thick * tiles * rows
+    for a in range(2):
+        for w in range(wide):
+            for z in range(thick):
+                for t in range(tiles):
+                    at = a * per + (z * tiles + t) * rows
+                    row = a * wide * thick + w * thick + z
+                    lanes = slice(t * LANES, (t + 1) * LANES)
+                    first[row : row + 1, lanes] = got[w, at : at + 1, :]
+                    last[row : row + 1, lanes] = got[w, at + rows - 1 : at + rows, :]
+
+
+def boil_body(dims, tab, got, lo, hi, smear, smear_e, fwd, c_x, shift,
+              source, mob, mob_lo, mob_hi, spec, message, outer, tp, pp, mass, heated, mask, entries):
+    wide, thick, rows, span, _ = dims
+    depth = wide * thick
+    tiles = span // LANES
+    per = thick * tiles * rows
+    size_x = smear_e.shape[0]
+    for w in range(wide):
+        entries[w : w + 1, :] = got[w, 2 * per : 2 * per + 1, :]
+        for z in range(thick):
+            for t in range(tiles):
+                at = (z * tiles + t) * rows
+                to = ((w * thick + z) * rows, t * LANES)
+                to = (slice(to[0], to[0] + rows), slice(to[1], to[1] + LANES))
+                tp[to] = got[w, at : at + rows, :]
+                pp[to] = got[w, per + at : per + at + rows, :]
+    for tx in range(span // size_x):
+        tile = (lax.axis_index("wide") * (span // size_x) + tx).astype(f32)
+        hit = jnp.where(entries[...] == tile, expansion, 0.0)
+        hit = jnp.max(hit, axis=1, keepdims=True)
+        mask[:, tx * size_x : (tx + 1) * size_x] = jnp.broadcast_to(hit, (wide, size_x))
+    mob[...] = jnp.where(pp[...] > 0.5, mobility_liquid, mobility_vapor)
+    mob_lo[...] = jnp.where(lo[depth:, :] > 0.5, mobility_liquid, mobility_vapor)
+    mob_hi[...] = jnp.where(hi[depth:, :] > 0.5, mobility_liquid, mobility_vapor)
+    r = lax.broadcasted_iota(jnp.int32, (rows, span), 0)
+    c = lax.broadcasted_iota(jnp.int32, (rows, span), 1)
+    own = lax.axis_index("narrow") * wide + lax.axis_index("wide")
+    no_lo, no_hi = own == 0, own == lax.axis_size("narrow") * wide - 1
+
+    def at_z(z):
+        return pl.ds(pl.multiple_of(z * rows, rows), rows)
+
+    def slab(z):
+        t, p = tp[at_z(z), :], pp[at_z(z), :]
+        below, above = at_z(jnp.maximum(z - 1, 0)), at_z(jnp.minimum(z + 1, depth - 1))
+
+        def along_y(x, k, up):
+            if up:
+                edge = jnp.where(no_hi, x[rows - 1 :], hi[pl.ds(k * depth + z, 1), :])
+                return jnp.where(r == rows - 1, edge, row_roll(x, True))
+            edge = jnp.where(no_lo, x[:1], lo[pl.ds(k * depth + z, 1), :])
+            return jnp.where(r == 0, edge, row_roll(x, False))
+
+        pairs = [
+            (tp[below, :], pp[below, :]),
+            (tp[above, :], pp[above, :]),
+            (along_y(t, 0, True), along_y(p, 1, True)),
+            (along_y(t, 0, False), along_y(p, 1, False)),
+            (jnp.where(c == span - 1, t, lane_roll(t, True)),
+             jnp.where(c == span - 1, p, lane_roll(p, True))),
+            (jnp.where(c == 0, t, lane_roll(t, False)),
+             jnp.where(c == 0, p, lane_roll(p, False))),
+        ]
+        heated[at_z(z), :], mass[at_z(z), :] = conducted(t, p, pairs)
+
+    lax.fori_loop(0, depth, lambda z, carry: (slab(z), carry)[1], 0)
+    for w in range(wide):
+        for k, z in enumerate((w * thick, (w + 1) * thick - 1)):
+            outer[w, k * rows : (k + 1) * rows, :] = heated[z * rows : (z + 1) * rows, :]
+    for tx in range(span // size_x):
+        at = slice(tx * size_x, (tx + 1) * size_x)
+        mass[:, at] = mat_t(mass[:, at], smear_e[...])
+    group = LANES
+    smear_n = smear_blocks(smear[...], group)
+    for g in range(depth * rows // group):
+        smeared = mat(smear_n, mass[g * group : (g + 1) * group, :])
+        for i in range(group // rows):
+            z = g * (group // rows) + i
+            source[z * rows : (z + 1) * rows, :] = (
+                smeared[i * rows : (i + 1) * rows] * mask[z // thick : z // thick + 1, :]
+            )
+    forward_body(
+        (depth, rows, span), tab, source, mass, spec, fwd, c_x, shift, message,
+        jnp.zeros((1, LANES), f32),
+    )
+
+
+def finish_body(dims, rho, parts, p, r, d, image, *refs):
+    outer, out = refs if len(refs) == 2 else (None, refs[0])
+    wide, thick, rows, span, _ = dims
+    total = parts[0]
+    for i in range(1, parts.shape[0]):
+        total = total + parts[i]
+    alpha = (rho[...] / jnp.sum(total, axis=1, keepdims=True))[:, :1]
+    n = thick * rows
+    for w in range(wide):
+        at = slice(w * n, (w + 1) * n)
+        out[w, :n, :] = p[at, :] + alpha * d[at, :]
+        out[w, n : 2 * n, :] = r[at, :] - alpha * image[at, :]
+        if outer is not None:
+            out[w, 2 * n :, :] = outer[w]
+
+
+def spread_body(dims, got, *refs):
+    wide, thick, rows, span, _ = dims
+    inner, outs = (refs[0], refs[1:]) if len(refs) == 4 else (None, refs)
+    for k, out in enumerate(outs):
+        for z in range(thick):
+            row = (k * thick + z) * rows
+            if k == 2:
+                if 0 < z < thick - 1:
+                    out[z] = inner[z - 1]
+                    continue
+                row = (2 * thick + (z > 0)) * rows
+            for w in range(wide):
+                out[z, w * rows : (w + 1) * rows, :] = got[w, row : row + rows, :]
 
 
 def forward_body(dims, tab, field, fold, spec, fwd, c_x, shift, message, extra):
@@ -246,10 +431,11 @@
     depth, rows, span = dims
     half = depth // 2
     if first_call:
-        (got, spec, shift, pair, sine, wave, h_new, message, low, high) = refs
+        (got, spec, shift, pairs, sine, wave, h_new, message, low, high) = refs
     else:
-        (got, spec, shift, pair, sine, wave, image_spec, h_old, rho,
+        (got, spec, shift, pairs, sine, wave, image_spec, h_old, rho,
          spec_new, h_new, message, alpha_out, low, high) = refs
+    pair = pairs[lax.axis_index("narrow") * lax.axis_size("wide") + lax.axis_index("wide")]
     for j in range(blocks):
         low[j : j + 1, :] = got[j, 0:1, :span]
         high[j : j + 1, :] = got[j, 0:1, span : 2 * span]
@@ -294,12 +480,18 @@
     size = half * rows
     refs = list(refs)
     take = refs.pop
+    if last_call:
+        n = ITERS - 1
+        at = 13
+        refs[at : at + 3 * n] = [refs[at : at + n], refs[at + n : at + 2 * n], refs[at + 2 * n : at + 3 * n]]
     got, spec, shift, inv, fwd, c_x, swap, mob, mob_lo, mob_hi = [take(0) for _ in range(10)]
     if not first_call:
         dir_old, q_old, rho_old = [take(0) for _ in range(3)]
+    if last_call:
+        alphas, olds, images, source = take(0), take(0), take(0), take(0)
     direction, image = take(0), take(0)
     if last_call:
-        rho_out, part_out = take(0), take(0)
+        rho_out, part_out, p_out, r_out = [take(0) for _ in range(4)]
     else:
         rho_out, dir_spec, q_out, image_spec, message = [take(0) for _ in range(5)]
     work, q_mid, fold = take(0), take(0), take(0)
@@ -375,24 +567,24 @@
     if last_call:
         for i in range(blocks):
             part_out[i] = part
+        p = alphas[0][:, :1] * olds[0][...]
+        r = source[...] - alphas[0][:, :1] * images[0][...]
+        for i in range(1, len(olds)):
+            p = p + alphas[i][:, :1] * olds[i][...]
+            r = r - alphas[i][:, :1] * images[i][...]
+        p_out[...] = p
+        r_out[...] = r
     else:
         forward_body(dims, tab, image, work, image_spec, fwd, c_x, shift, message, part)
 
 
-def on_device(superheat_excess, liquid_indicator, listing, smear_n, smear_e):
+def split_by_z(superheat_excess, liquid_indicator, listing, smear_n, smear_e, dims, const):
     thick, north, span = superheat_excess.shape
     wide, lanes = lax.axis_size("wide"), lax.axis_size("narrow")
-    w, n = lax.axis_index("wide"), lax.axis_index("narrow")
-    blocks = wide * lanes
-    depth = thick * wide
-    rows = north // wide
+    depth, rows, span = dims[1]
     size_y, size_x = smear_n.shape[0], smear_e.shape[0]
     tiles_y = north // size_y
-    dims = (depth, rows, span)
-    tab = tables(depth, rows, span, blocks)
-    own = n * wide + w
     whole = depth * rows
-
     phase = liquid_indicator.astype(f32)
     both = jnp.stack([superheat_excess, phase])
     up = [(i, i + 1) for i in range(wide - 1)]
@@ -411,27 +603,14 @@
     mob = jnp.where(phase > 0.5, mobility_liquid, mobility_vapor)
     mob = mob.reshape(thick, wide, rows, span).transpose(1, 0, 2, 3)
     mob = regroup(mob).reshape(depth, rows, span)
-
-    def place(j):
-        return (j % wide) * lanes + j // wide
-
-    up = [(place(j), place(j + 1)) for j in range(blocks - 1)]
-    down = [(b, a) for a, b in up]
-    mob_lo = lax.ppermute(mob[:, rows - 1], ("wide", "narrow"), up)
-    mob_hi = lax.ppermute(mob[:, 0], ("wide", "narrow"), down)
-    mob = mob.reshape(whole, span)
-
-    pos = jnp.stack([w, wide - 1 - w, n, lanes - 1 - n]).astype(jnp.int32)
-    blockn = (jnp.eye(tiles_y, dtype=f32)[:, None, :, None] * smear_n[None, :, None, :]).reshape(
-        north, north
-    )
     most = listing.size
     heat_dims = (thick, north, span, size_y, size_x, most)
     heated, source = call(
         lambda *r: heat_body(heat_dims, *r),
         [(thick, north, span), (tiles_y, thick, size_y, span)],
-        pos, listing.reshape(-1), superheat_excess, liquid_indicator, zlo, zhi, ylo, yhi, blockn, smear_e,
-        smem=(0, 1),
+        listing.reshape(-1), superheat_excess, liquid_indicator, zlo, zhi, ylo, yhi,
+        smear_n, smear_e,
+        smem=(0,),
         scratch=[
             VMEM((thick + 2, north, span), f32),
             VMEM((thick + 2, north, span), f32),
@@ -440,67 +619,155 @@
         ],
         name="heat",
     )
+    source, mob = lax.optimization_barrier((source, mob))
     if size_y != rows:
         source = source.transpose(1, 0, 2, 3).reshape(thick, wide, rows, span).transpose(1, 0, 2, 3)
     source = regroup(source).reshape(whole, span)
-
-    c_x, fwd, inv = (jnp.asarray(tab[k]) for k in ("c_x", "forward", "inverse"))
-    swap, shift, sine, wave = (jnp.asarray(tab[k]) for k in ("swap", "shift", "sine", "wave"))
-    pair = lax.dynamic_index_in_dim(jnp.asarray(tab["pair"]), own, 0, keepdims=False)
-    full = (whole, span)
+    up, down = const["row_pairs"]
+    mob_lo = lax.ppermute(mob[:, rows - 1], ("wide", "narrow"), up)
+    mob_hi = lax.ppermute(mob[:, 0], ("wide", "narrow"), down)
+    spec, message = call(
+        lambda *r: start_body(dims[1], const["tab"], *r), [(whole, span), const["letter"]],
+        source, const["forward"], const["c_x"], const["shift"],
+        scratch=[VMEM((whole, span), f32)], name="start",
+    )
+    return heated, source, mob.reshape(whole, span), mob_lo, mob_hi, spec, message
+
+
+def split_by_y(superheat_excess, liquid_indicator, listing, smear_n, smear_e, dims, const):
+    depth, rows, span = dims[1]
+    wide, thick = dims[0][:2]
+    whole = depth * rows
+    per = thick * rows * (span // LANES)
+    north = superheat_excess.shape[1]
+    packed, side_first, side_last = call(
+        lambda *r: pack_body(dims[0], *r),
+        [(wide, 2 * per + 8, LANES), (2, thick, 1, span), (2, thick, 1, span)],
+        listing, superheat_excess, liquid_indicator, far=(1, 2),
+        scratch=[
+            VMEM((thick, north, span), f32),
+            VMEM((thick, north, span), jnp.int32),
+            VMEM((8, LANES), f32),
+            pltpu.SemaphoreType.DMA((2,)),
+        ],
+        name="pack",
+    )
+    got = lax.all_to_all(packed, "wide", split_axis=0, concat_axis=0, tiled=True)
+    first, last = call(lambda *r: edge_body(dims[0], *r), [(2 * depth, span)] * 2, got, name="edge")
+    up, down = const["row_pairs"]
+    lo = lax.ppermute(last, ("wide", "narrow"), up)
+    hi = lax.ppermute(first, ("wide", "narrow"), down)
+    full, plane = (whole, span), (depth, span)
+    return side_first, side_last, *call(
+        lambda *r: boil_body(dims[0], const["tab"], *r),
+        [full, full, plane, plane, full, const["letter"], (wide, 2 * rows, span)],
+        got, lo, hi, smear_n, smear_e, const["forward"], const["c_x"], const["shift"],
+        scratch=[VMEM(full, f32)] * 4 + [VMEM((wide, span), f32), VMEM((wide, LANES), f32)],
+        name="boil",
+    )
+
+
+def on_device(superheat_excess, liquid_indicator, listing, smear_n, smear_e):
+    thick, north, span = superheat_excess.shape
+    wide, lanes = lax.axis_size("wide"), lax.axis_size("narrow")
+    blocks = wide * lanes
+    depth = thick * wide
+    rows = north // wide
+    size_y = smear_n.shape[0]
+    shape = (depth, rows, span)
+    dims = ((wide, thick, rows, span, listing.size), shape)
+    tab = tables(depth, rows, span, blocks)
+    whole = depth * rows
+    full, one = (whole, span), (1, LANES)
     letter = (blocks, 1, 2 * span + LANES)
-    one = (1, LANES)
+
+    def place(j):
+        return (j % wide) * lanes + j // wide
+
+    up = [(place(j), place(j + 1)) for j in range(blocks - 1)]
+    const = {k: jnp.asarray(tab[k]) for k in ("c_x", "forward", "inverse", "swap", "shift", "pair", "sine", "wave")}
+    const["tab"], const["letter"] = tab, letter
+    const["row_pairs"] = up, [(b, a) for a, b in up]
+    by_y = rows == size_y and thick > 2
+    if by_y:
+        side_first, side_last, source, mob, mob_lo, mob_hi, spec, message, outer = split_by_y(
+            superheat_excess, liquid_indicator, listing, smear_n, smear_e, dims, const
+        )
+    else:
+        heated, source, mob, mob_lo, mob_hi, spec, message = split_by_z(
+            superheat_excess, liquid_indicator, listing, smear_n, smear_e, dims, const
+        )
 
     def swap_all(x):
         return lax.all_to_all(x, ORDER, split_axis=0, concat_axis=0, tiled=True)
 
-    spec, message = call(
-        lambda *r: start_body(dims, tab, *r), [full, letter], source, fwd, c_x, shift,
-        scratch=[VMEM(full, f32)], name="start",
-    )
+    shift, pair, sine, wave = (const[k] for k in ("shift", "pair", "sine", "wave"))
     pair_scratch = [VMEM((blocks, span), f32)] * 2
     jump, message = call(
-        lambda *r: solve_body(dims, tab, True, blocks, *r), [(blocks, span), letter],
-        swap_all(message), spec, shift, pair, sine, wave, scratch=pair_scratch, name="solve",
-    )
-    pressure, residual = None, source
+        lambda *r: solve_body(shape, tab, True, blocks, *r), [(blocks, span), letter],
+        swap_all(message), spec, shift, pair, sine, wave, scratch=pair_scratch,
+        name="solve",
+    )
     dir_spec = q = rho = None
+    directions, images, alphas = [], [], []
     for iteration in range(ITERS):
         first, final = iteration == 0, iteration + 1 == ITERS
-        args = [swap_all(message), spec, shift, inv, fwd, c_x, swap, mob, mob_lo, mob_hi]
+        args = [swap_all(message), spec, shift, const["inverse"], const["forward"], const["c_x"], const["swap"], mob, mob_lo, mob_hi]
         if not first:
             args += [dir_spec, q, rho]
         outs = [full, full, one]
         work = [VMEM(full, f32), VMEM((2 * depth, span), f32), VMEM(full, f32)]
         if final:
-            outs += [(blocks, 1, LANES)]
+            outs += [(blocks, 1, LANES), full, full]
+            args += [*alphas, *directions, *images, source]
             work += [VMEM(full, f32), VMEM((2 * depth, span), f32)]
         else:
             outs += [full, (2 * depth, span), full, letter]
         result = call(
-            lambda *r, a=first, b=final: advance_body(dims, tab, a, b, blocks, *r), outs, *args,
+            lambda *r, a=first, b=final: advance_body(shape, tab, a, b, blocks, *r), outs, *args,
             scratch=work, name="advance",
         )
-        direction, image, rho = result[:3]
+        directions.append(result[0])
+        images.append(result[1])
+        rho = result[2]
         if final:
-            bottom = jnp.sum(swap_all(result[3]))
-            alpha = rho[0, 0] / bottom
+            parts = swap_all(result[3])
+            pressure, residual = result[4:]
         else:
             dir_spec, q, image_spec, message = result[3:]
             spec, jump, message, alpha = call(
-                lambda *r: solve_body(dims, tab, False, blocks, *r),
+                lambda *r: solve_body(shape, tab, False, blocks, *r),
                 [full, (blocks, span), letter, one],
                 swap_all(message), spec, shift, pair, sine, wave, image_spec, jump, rho,
                 scratch=pair_scratch, name="solve",
             )
-            alpha = alpha[0, 0]
-        pressure = alpha * direction if first else pressure + alpha * direction
-        residual = residual - alpha * image
-
-    both = jnp.stack([pressure, residual]).reshape(2, wide, thick, rows, span)
-    both = lax.all_to_all(both, "wide", split_axis=1, concat_axis=1, tiled=True)
-    both = both.transpose(0, 2, 1, 3, 4).reshape(2, thick, north, span)
-    return heated, both[0], both[1]
+            alphas.append(alpha)
+
+    extra = [outer] if by_y else []
+    (both,) = call(
+        lambda *r: finish_body(dims[0], *r), [(wide, 2 * (thick + len(extra)) * rows, span)],
+        rho, parts, pressure, residual, directions[2], images[2], *extra, name="finish",
+    )
+    both = lax.all_to_all(both, "wide", split_axis=0, concat_axis=0, tiled=True)
+    outs = [(thick, north, span)] * (2 + len(extra))
+    if not by_y:
+        pressure, residual = call(
+            lambda *r: spread_body(dims[0], *r), outs, both, name="spread"
+        )
+        return heated, pressure, residual
+    y_up = [(i, i + 1) for i in range(lanes - 1)]
+    y_down = [(i + 1, i) for i in range(lanes - 1)]
+    ylo = lax.ppermute(side_last, "narrow", y_up)
+    yhi = lax.ppermute(side_first, "narrow", y_down)
+    (inner,) = call(
+        lambda *r: heat_body((thick, north, span, size_y, span, 0), *r),
+        [(thick - 2, north, span)], superheat_excess, liquid_indicator, ylo, yhi,
+        scratch=[VMEM((thick, north, span), f32)], name="heat",
+    )
+    pressure, residual, heated = call(
+        lambda *r: spread_body(dims[0], *r), outs, both, inner, name="spread"
+    )
+    return heated, pressure, residual
 
 
 def solution(mesh):

time: 277 us -> 250 us (0.903)
  starting transfers between devices: 26.7 us -> 10.7 us
  local copies, waits for them, and re-layouts: 18.6 us -> 5.6 us
  waiting for transfers between devices: 50.1 us -> 59 us
  other arithmetic: 7.64 us -> 0 us
  Pallas kernels: 33.5 us -> 39.9 us
  blocking collectives: 138 us -> 133 us
    all_to_all x2 -> x1, blocking collectives: 82.4 us -> 56.8 us  [split_by_y(): lax.all_to_all(packed, 'wide', split_axis=0, concat_axis=0, tiled=True)]
    all_to_all x3 -> x1, waiting for transfers between devices: 29.1 us -> 51 us  [on_device(): both = lax.all_to_all(both, 'wide', split_axis=0, concat_axis=0, tiled=True)]
    all_to_all x5 -> x7, blocking collectives: 55.2 us -> 76.6 us  [swap_all(): return lax.all_to_all(x, ORDER, split_axis=0, concat_axis=0, tiled=True)]
    ppermute x6 -> x4, waiting for transfers between devices: 20.9 us -> 8.02 us  [the longest x1 4.68 us: split_by_y(): hi = lax.ppermute(first, ('wide', 'narrow'), down)]
    ppermute x6 -> x4, starting transfers between devices: 16.4 us -> 7.06 us  [the longest x1 2.74 us: split_by_y(): lo = lax.ppermute(last, ('wide', 'narrow'), up)]
    unnamed x64 -> x30, local copies, waits for them, and re-layouts: 14.7 us -> 5.6 us
    all_to_all x3 -> x1, starting transfers between devices: 10.3 us -> 3.63 us  [on_device(): both = lax.all_to_all(both, 'wide', split_axis=0, concat_axis=0, tiled=True)]
    pallas_call x8 -> x12, Pallas kernels: 33.5 us -> 39.9 us  [call(): pl.pallas_call(body, out_shape=[jax.ShapeDtypeStruct(s, f32) for s in out...]
  transfers between devices with their start and end apart: 9 -> 5, of which waited for: 7 -> 4; matrix products, arithmetic and copies ran while one was open for 1% -> 0% of each run, Pallas kernels for 0% -> 0%
where the time goes in v2:
time: 250 us; the launch traced here: 249 us
  blocking collectives  133 us (53%)
  waiting for transfers between devices  59 us (24%)
  Pallas kernels  39.9 us (16%)
  starting transfers between devices  10.7 us (4%)
  local copies, waits for them, and re-layouts  5.6 us (2%)
    all_to_all x7, blocking collectives, swap_all(): return lax.all_to_all(x, ORDER, split_axis=0, concat_axis=0, tiled=True)  76.6 us
    all_to_all x1, blocking collectives, split_by_y(): lax.all_to_all(packed, 'wide', split_axis=0, concat_axis=0, tiled=True)  56.8 us
    all_to_all x1, waiting for transfers between devices, on_device(): both = lax.all_to_all(both, 'wide', split_axis=0, concat_axis=0, tiled=True)  51 us
    pallas_call x12, Pallas kernels, call(): pl.pallas_call(body, out_shape=[jax.ShapeDtypeStruct(s, f32) for s in out...  39.9 us
    unnamed x30, local copies, waits for them, and re-layouts  5.6 us
  transfers between devices with their start and end apart: 5, of which 4 were waited for; matrix products, arithmetic and copies ran while one was open for 0% of the time, Pallas kernels for 0%

profile of v2, /device:TPU:0, one launch (start us, length us, event | category | flops | bytes accessed | tf_op | source)
XLA Modules:
  0.0 249.5 jit_solution(14409345845964174749)
XLA Ops:
  0.6 1.2 copy-done.7
  1.9 1.2 copy-done.9
  3.1 0.7 copy-done.11
  4.1 56.8 %all_to_all.45.r_0_ = f32[8,520,128]{2,1,0:T(8,128)S(1)} all-to-all(f32[8,520,128]{2,1,0:T(8,128)S(1)} %get-tuple-element.47), channel_id=1, replica_groups=mesh['wide'=8,'narrow'=4] {'wide'}, dimensions={0} | all-to-all | bytes 4259840 | tf_op jit(solution)/shard_map/all_to_all | solution.py:655
  61.1 2.7 %collective-permute-start = (f32[64,512]{1,0:T(8,128)S(1)}, f32[64,512]{1,0:T(8,128)S(1)}, u32[]{:S(2)}, u32[]{:S(2)}) collective-permute-start(f32[64,512]{1,0:T(8,128)S(1)} %get-tuple-element.48), channel_id=1, source_target_pairs={{0,4},{4,8},{8,12},{12,16},{16,20},{20,24},{24,28},{28,1},{1,5},{5... | collective-permute-start | bytes 393224 | tf_op jit(solution)/shard_map/ppermute | solution.py:658
  63.8 1.3 collective-permute-start.1
  65.1 1.2 collective-permute-done.r_1_
  66.3 4.7 %collective-permute-done.1.r_2_ = f32[64,512]{1,0:T(8,128)S(1)} collective-permute-done((f32[64,512]{1,0:T(8,128)S(1)}, f32[64,512]{1,0:T(8,128)S(1)}, u32[]{:S(2)}, u32[]{:S(2)}) %collective-permute-start.1) | collective-permute-done | bytes 131104 | tf_op jit(solution)/shard_map/ppermute | solution.py:659
  71.0 9.3 %boil.1 = (f32[512,512]{1,0:T(8,128)S(1)}, f32[512,512]{1,0:T(8,128)S(1)}, f32[32,512]{1,0:T(8,128)S(1)}, f32[32,512]{1,0:T(8,128)S(1)}, f32[512,512]{1,0:T(8,12...) custom-call(f32[8,520,128]{2,1,0:T(8,128)S(1)} %all_to_all.45.r_0_, ...), custom_call_target="tpu_custom_call" | custom-call | flops 1000000000 | bytes 4194304 | tf_op jit(solution)/shard_map/boil/pallas_call | solution.py:97
  80.3 15.5 %all_to_all.46.r_0_ = f32[32,1,1152]{2,1,0:T(1,128)S(1)} all-to-all(f32[32,1,1152]{2,1,0:T(1,128)S(1)} %get-tuple-element.50), channel_id=1, replica_groups=mesh['wide'=8,'narrow'=4] {'narrow','wide'}, dimensions={0} | all-to-all | bytes 294912 | tf_op jit(solution)/shard_map/all_to_all | solution.py:702
  95.8 0.5 solve.3
  96.3 10.3 %all_to_all.47.r_0_ = f32[32,1,1152]{2,1,0:T(1,128)S(1)} all-to-all(f32[32,1,1152]{2,1,0:T(1,128)S(1)} %get-tuple-element.52), channel_id=1, replica_groups=mesh['wide'=8,'narrow'=4] {'narrow','wide'}, dimensions={0} | all-to-all | bytes 294912 | tf_op jit(solution)/shard_map/all_to_all | solution.py:702
  106.6 8.5 %advance.3 = (f32[512,512]{1,0:T(8,128)S(1)}, f32[512,512]{1,0:T(8,128)S(1)}, f32[1,128]{1,0:T(1,128)S(1)}, f32[512,512]{1,0:T(8,128)S(1)}, f32[64,512]{1,0:T(8,...) custom-call(f32[32,1,1152]{2,1,0:T(1,128)S(1)} %all_to_all.47.r_0_, f32[512,512]{1,0:T(8,128)S(1)} %get-tuple-element.51.r_1_, ...), custom_call_target="tpu_custom_call" | custom-call | flops 1000000000 | bytes 4194304 | tf_op jit(solution)/shard_map/advance/pallas_call | solution.py:97
  115.1 10.3 %all_to_all.48.r_0_ = f32[32,1,1152]{2,1,0:T(1,128)S(1)} all-to-all(f32[32,1,1152]{2,1,0:T(1,128)S(1)} %get-tuple-element.56), channel_id=1, replica_groups=mesh['wide'=8,'narrow'=4] {'narrow','wide'}, dimensions={0} | all-to-all | bytes 294912 | tf_op jit(solution)/shard_map/all_to_all | solution.py:702
  125.5 0.6 solve.4
  126.1 10.3 %all_to_all.49.r_0_ = f32[32,1,1152]{2,1,0:T(1,128)S(1)} all-to-all(f32[32,1,1152]{2,1,0:T(1,128)S(1)} %get-tuple-element.60), channel_id=1, replica_groups=mesh['wide'=8,'narrow'=4] {'narrow','wide'}, dimensions={0} | all-to-all | bytes 294912 | tf_op jit(solution)/shard_map/all_to_all | solution.py:702
  136.4 8.5 %advance.4 = (f32[512,512]{1,0:T(8,128)S(1)}, f32[512,512]{1,0:T(8,128)S(1)}, f32[1,128]{1,0:T(1,128)S(1)}, f32[512,512]{1,0:T(8,128)S(1)}, f32[64,512]{1,0:T(8,...) custom-call(f32[32,1,1152]{2,1,0:T(1,128)S(1)} %all_to_all.49.r_0_, f32[512,512]{1,0:T(8,128)S(1)} %get-tuple-element.61.r_1_, ...), custom_call_target="tpu_custom_call" | custom-call | flops 1000000000 | bytes 4194304 | tf_op jit(solution)/shard_map/advance/pallas_call | solution.py:97
  144.9 10.3 %all_to_all.50.r_0_ = f32[32,1,1152]{2,1,0:T(1,128)S(1)} all-to-all(f32[32,1,1152]{2,1,0:T(1,128)S(1)} %get-tuple-element.64), channel_id=1, replica_groups=mesh['wide'=8,'narrow'=4] {'narrow','wide'}, dimensions={0} | all-to-all | bytes 294912 | tf_op jit(solution)/shard_map/all_to_all | solution.py:702
  155.2 1.1 solve.5
  156.4 10.3 %all_to_all.51.r_0_ = f32[32,1,1152]{2,1,0:T(1,128)S(1)} all-to-all(f32[32,1,1152]{2,1,0:T(1,128)S(1)} %get-tuple-element.68), channel_id=1, replica_groups=mesh['wide'=8,'narrow'=4] {'narrow','wide'}, dimensions={0} | all-to-all | bytes 294912 | tf_op jit(solution)/shard_map/all_to_all | solution.py:702
  166.7 6.1 %advance.5 = (f32[512,512]{1,0:T(8,128)S(1)}, f32[512,512]{1,0:T(8,128)S(1)}, f32[1,128]{1,0:T(1,128)S(1)}, f32[32,1,128]{2,1,0:T(1,128)S(1)}, f32[512,512]{1,0:T(8,128)S(1)}, /*index=5*/f32[512,512]{1,0:T(8,128)S(1)}) custom-call(f32[32,1,1152]{2,1,0:T(1,128)S(1)} %all_to_all.51.r_0_, f32[512,512]{1,0:T(8,128)S(1)} %get-tuple-element.69.r_1_, ...), custom_call_target="tpu_custom_call" | custom-call | flops 1000000000 | bytes 4194304 | tf_op jit(solution)/shard_map/advance/pallas_call | solution.py:97
  172.8 9.6 %all_to_all.52.r_1_ = f32[32,1,128]{2,1,0:T(1,128)S(1)} all-to-all(f32[32,1,128]{2,1,0:T(1,128)S(1)} %get-tuple-element.80), channel_id=1, replica_groups=mesh['wide'=8,'narrow'=4] {'narrow','wide'}, dimensions={0} | all-to-all | bytes 32768 | tf_op jit(solution)/shard_map/all_to_all | solution.py:702
  182.3 2.0 finish.1
  184.3 3.6 %all-to-all-start.8 = ((f32[8,160,512]{2,1,0:T(8,128)}), f32[8,160,512]{2,1,0:T(8,128)S(1)}, u32[]{:S(2)}, u32[]{:S(2)}) async-start(f32[8,160,512]{2,1,0:T(8,128)} %finish.1), calls=%async_computation.8 | async-start | bytes 5242880 | tf_op jit(solution)/shard_map/all_to_all | solution.py:751
  187.9 1.7 collective-permute-start.2
  189.7 1.3 collective-permute-start.3
  191.0 2.1 collective-permute-done.3.r_3_
  193.1 1.2 copy-done.8
  194.4 1.2 copy-done.10
  195.6 1.0 heat.1.r_1_
  196.6 51.0 %all-to-all-done.8.r_0_ = f32[8,160,512]{2,1,0:T(8,128)S(1)} async-done(((f32[8,160,512]{2,1,0:T(8,128)}), f32[8,160,512]{2,1,0:T(8,128)S(1)}, u32[]{:S(2)}, u32[]{:S(2)}) %all-to-all-start.8) | async-done | bytes 2621472 | tf_op jit(solution)/shard_map/all_to_all | solution.py:751
  247.6 1.9 spread.1
  (28 shorter events, 0.6 us)
Async XLA Ops:
  0.6 1.2 copy-start.7
  1.9 1.2 copy-start.9
  3.1 0.7 copy-start.11
  60.8 10.2 %copy-start = (f32[512,512]{1,0:T(8,128)S(1)}, f32[512,512]{1,0:T(8,128)}, u32[]{:S(2)}) copy-start(f32[512,512]{1,0:T(8,128)} %constant.16.clone.r_6_.r_5_) | copy-start | bytes 3145732
  60.8 10.2 %copy-start.1 = (f32[2,256,256]{2,1,0:T(8,128)S(1)}, f32[2,256,256]{2,1,0:T(8,128)}, u32[]{:S(2)}) copy-start(f32[2,256,256]{2,1,0:T(8,128)} %constant.17.clone.r_5_.r_4_) | copy-start | bytes 1572868
  60.8 10.2 %copy-start.3 = (f32[32,512]{1,0:T(8,128)S(1)}, f32[32,512]{1,0:T(8,128)}, u32[]{:S(2)}) copy-start(f32[32,512]{1,0:T(8,128)} %constant.20.clone.r_7_.r_2_) | copy-start | bytes 196612
  60.8 10.2 %copy-start.5 = (f32[128,128]{1,0:T(8,128)S(1)}, f32[128,128]{1,0:T(8,128)}, u32[]{:S(2)}) copy-start(f32[128,128]{1,0:T(8,128)} %r_4_.7) | copy-start | bytes 196612
  60.8 10.2 %copy-start.6 = (f32[16,16]{1,0:T(8,128)S(1)}, f32[16,16]{1,0:T(8,128)}, u32[]{:S(2)}) copy-start(f32[16,16]{1,0:T(8,128)} %r_3_.7) | copy-start | bytes 3076
  61.0 34.7 %copy-start.12 = (f32[32,2,512]{2,1,0:T(2,128)S(1)}, f32[32,2,512]{2,1,0:T(2,128)}, u32[]{:S(2)}) copy-start(f32[32,2,512]{2,1,0:T(2,128)} %constant.21.clone.r_3_) | copy-start | bytes 393220
  61.1 34.7 %copy-start.13 = (f32[32,32]{1,0:T(8,128)S(1)}, f32[32,32]{1,0:T(8,128)}, u32[]{:S(2)}) copy-start(f32[32,32]{1,0:T(8,128)} %constant.22.clone.r_4_) | copy-start | bytes 12292
  61.1 34.7 %copy-start.14 = (f32[32,128]{1,0:T(8,128)S(1)}, f32[32,128]{1,0:T(8,128)}, u32[]{:S(2)}) copy-start(f32[32,128]{1,0:T(8,128)} %constant.23.clone.r_5_) | copy-start | bytes 49156
  61.1 5.2 %collective-permute-start = (f32[64,512]{1,0:T(8,128)S(1)}, f32[64,512]{1,0:T(8,128)S(1)}, u32[]{:S(2)}, u32[]{:S(2)}) collective-permute-start(f32[64,512]{1,0:T(8,128)S(1)} %get-tuple-element.48), channel_id=1, source_target_pairs={{0,4},{4,8},{8,12},{12,16},{16,20},{20,24},{24,28},{28,1},{1,5},{5... | collective-permute-start | bytes 393224 | tf_op jit(solution)/shard_map/ppermute | solution.py:658
  63.8 7.2 %collective-permute-start.1 = (f32[64,512]{1,0:T(8,128)S(1)}, f32[64,512]{1,0:T(8,128)S(1)}, u32[]{:S(2)}, u32[]{:S(2)}) collective-permute-start(f32[64,512]{1,0:T(8,128)S(1)} %get-tuple-element.49), channel_id=1, source_target_pairs={{4,0},{8,4},{12,8},{16,12},{20,16},{24,20},{28,24},{1,28},{5,1},{9... | collective-permute-start | bytes 393224 | tf_op jit(solution)/shard_map/ppermute | solution.py:659
  80.3 26.3 %copy-start.2 = (f32[2,256,256]{2,1,0:T(8,128)S(1)}, f32[2,256,256]{2,1,0:T(8,128)}, u32[]{:S(2)}) copy-start(f32[2,256,256]{2,1,0:T(8,128)} %constant.18.clone.r_3_) | copy-start | bytes 1572868
  80.3 26.3 %copy-start.4 = (f32[64,64]{1,0:T(8,128)S(1)}, f32[64,64]{1,0:T(8,128)}, u32[]{:S(2)}) copy-start(f32[64,64]{1,0:T(8,128)} %constant.19.clone.r_6_) | copy-start | bytes 49156
  184.3 63.3 %all-to-all-start.8 = ((f32[8,160,512]{2,1,0:T(8,128)}), f32[8,160,512]{2,1,0:T(8,128)S(1)}, u32[]{:S(2)}, u32[]{:S(2)}) async-start(f32[8,160,512]{2,1,0:T(8,128)} %finish.1), calls=%async_computation.8 | async-start | bytes 5242880 | tf_op jit(solution)/shard_map/all_to_all | solution.py:751
  187.9 3.1 %collective-permute-start.2 = (f32[2,4,1,512]{3,2,1,0:T(1,128)S(1)}, f32[2,4,1,512]{3,2,1,0:T(1,128)S(1)}, u32[]{:S(2)}, u32[]{:S(2)}) collective-permute-start(f32[2,4,1,512]{3,2,1,0:T(1,128)S(1)} %get-tuple-element.86), channel_id=1, source_target_pairs={{0,1},{1,2},{2,3},{4,5},{5,6},{6,7},{8,9},{9,10},{10,11},{12,13},{... | collective-permute-start | bytes 49160 | tf_op jit(solution)/shard_map/ppermute | solution.py:760
  189.7 3.5 %collective-permute-start.3 = (f32[2,4,1,512]{3,2,1,0:T(1,128)S(1)}, f32[2,4,1,512]{3,2,1,0:T(1,128)S(1)}, u32[]{:S(2)}, u32[]{:S(2)}) collective-permute-start(f32[2,4,1,512]{3,2,1,0:T(1,128)S(1)} %get-tuple-element.87), channel_id=1, source_target_pairs={{1,0},{2,1},{3,2},{5,4},{6,5},{7,6},{9,8},{10,9},{11,10},{13,12},{... | collective-permute-start | bytes 49160 | tf_op jit(solution)/shard_map/ppermute | solution.py:761
  193.1 1.2 copy-start.8
  194.4 1.2 copy-start.10

commit v3 on v2

--- a/solution.py
+++ b/solution.py
@@ -7,6 +7,7 @@
 from jax.experimental import pallas as pl
 from jax.experimental.pallas import tpu as pltpu
 from jax.sharding import PartitionSpec as P
+
 
 ITERS = 3
 
@@ -89,7 +90,7 @@
     }
 
 
-def call(body, outs, *args, smem=(), far=(), scratch=(), flops=1e9, name=None):
+def call(body, outs, *args, smem=(), far=(), far_out=False, scratch=(), flops=1e9):
     specs = [
         pl.BlockSpec(memory_space=pltpu.SMEM if i in smem else pl.ANY if i in far else VMEM)
         for i in range(len(args))
@@ -98,20 +99,11 @@
         body,
         out_shape=[jax.ShapeDtypeStruct(s, f32) for s in outs],
         in_specs=specs,
-        out_specs=[pl.BlockSpec(memory_space=VMEM)] * len(outs),
+        out_specs=[pl.BlockSpec(memory_space=pl.ANY if far_out else VMEM)] * len(outs),
         scratch_shapes=list(scratch),
         compiler_params=pltpu.CompilerParams(vmem_limit_bytes=16 * 2**20),
         cost_estimate=pl.CostEstimate(flops=int(flops), bytes_accessed=4 << 20, transcendentals=0),
-        name=name,
     )(*args)
-
-
-def step(count, aligned, body):
-    if aligned:
-        lax.fori_loop(0, count, lambda i, c: (body(i), c)[1], 0)
-    else:
-        for i in range(count):
-            body(i)
 
 
 def row_roll(x, up):
@@ -161,37 +153,40 @@
     return value, 2.0 * k * faces * value
 
 
-def heat_body(dims, *refs):
+def heat_body(dims, inner, *refs):
     thick, north, span, size_y, size_x, most = dims
-    with_source = most > 0
-    if with_source:
+    if inner:
+        (table, temp, phase, ylo, yhi, smear, smear_e, heated, source, mob, pp, mass, mask) = refs
+        tp = temp
+    else:
         (table, temp, phase, zlo, zhi, ylo, yhi, smear, smear_e,
          heated, source, tp, pp, mass, mask) = refs
-    else:
-        temp, phase, ylo, yhi, heated, pp = refs
-        tp = temp
-    base = 1 if with_source else 0
+    skip = 1 if inner else 0
+    base = 1 - skip
+    planes = thick - 2 * skip
     tiles_y = north // size_y
     tiles_x = span // size_x
     w, n = lax.axis_index("wide"), lax.axis_index("narrow")
     n_first, n_last = n == 0, n == lax.axis_size("narrow") - 1
     for z in range(thick):
         pp[z + base] = phase[z].astype(f32)
-    if with_source:
+        if inner:
+            mob[z] = jnp.where(pp[z] > 0.5, mobility_liquid, mobility_vapor)
+        else:
+            tp[z + 1] = temp[z]
+    if not inner:
         w_first, w_last = w == 0, w == lax.axis_size("wide") - 1
-        for z in range(thick):
-            tp[z + 1] = temp[z]
         tp[0] = jnp.where(w_first, temp[0], zlo[0])
         pp[0] = jnp.where(w_first, phase[0].astype(f32), zlo[1])
         tp[thick + 1] = jnp.where(w_last, temp[thick - 1], zhi[0])
         pp[thick + 1] = jnp.where(w_last, phase[thick - 1].astype(f32), zhi[1])
-        row = lax.broadcasted_iota(jnp.int32, (tiles_y, span), 0)
-        lane = lax.broadcasted_iota(jnp.int32, (tiles_y, span), 1)
-        tile = row * tiles_x + lane // size_x
-        hit = tile == table[0]
-        for i in range(1, most):
-            hit = jnp.logical_or(hit, tile == table[i])
-        mask[...] = jnp.where(hit, expansion, 0.0)
+    row = lax.broadcasted_iota(jnp.int32, (tiles_y, span), 0)
+    lane = lax.broadcasted_iota(jnp.int32, (tiles_y, span), 1)
+    tile = row * tiles_x + lane // size_x
+    hit = tile == table[0]
+    for i in range(1, most):
+        hit = jnp.logical_or(hit, tile == table[i])
+    mask[...] = jnp.where(hit, expansion, 0.0)
     r = lax.broadcasted_iota(jnp.int32, (size_y, span), 0)
     c = lax.broadcasted_iota(jnp.int32, (size_y, span), 1)
 
@@ -225,23 +220,23 @@
                 jnp.where(r == 0, edge(pp, ylo, 1, y, n_first, p[:1]), row_roll(p, False)),
             ))
             value, vapor = conducted(t, p, pairs)
-            heated[z if with_source else z - 1, at, :] = value
-            if with_source:
-                to = pl.ds(pl.multiple_of(z * north, north) + yc * size_y, size_y)
-                mass[to, :] = vapor
-
-    inner = 1 - base
-    lax.fori_loop(inner, thick - inner, lambda z, carry: (plane(z), carry)[1], 0)
-    if not with_source:
-        return
+            heated[z - skip, at, :] = value
+            to = pl.ds(pl.multiple_of((z - skip) * north, north) + yc * size_y, size_y)
+            mass[to, :] = vapor
+
+    lax.fori_loop(skip, thick - skip, lambda z, carry: (plane(z), carry)[1], 0)
     smear_n = smear_blocks(smear[...], north)
     for tx in range(tiles_x):
         at = slice(tx * size_x, (tx + 1) * size_x)
         mass[:, at] = mat_t(mass[:, at], smear_e[...])
-    for z in range(thick):
+    for z in range(planes):
         smeared = mat(smear_n, mass[z * north : (z + 1) * north, :])
         for yc in range(tiles_y):
-            source[yc, z] = smeared[yc * size_y : (yc + 1) * size_y] * mask[yc : yc + 1, :]
+            part = smeared[yc * size_y : (yc + 1) * size_y] * mask[yc : yc + 1, :]
+            if inner:
+                source[z, yc * size_y : (yc + 1) * size_y, :] = part
+            else:
+                source[yc, z] = part
 
 
 def pack_body(dims, listing, far_temp, far_phase, out, side_first, side_last, temp, phase, entry, sems):
@@ -257,6 +252,7 @@
         copy.start()
     entry[...] = jnp.full((8, LANES), -1.0, f32)
     entry[0:1, 0:most] = listing[0].astype(f32)
+    odd = lax.axis_index("narrow") % 2 == 1
     for w in range(wide):
         out[w, 2 * per :, :] = entry[...]
     for a, ref in enumerate((temp, phase)):
@@ -268,7 +264,7 @@
                 for t in range(tiles):
                     at = a * per + (z * tiles + t) * rows
                     piece = ref[z, w * rows : (w + 1) * rows, t * LANES : (t + 1) * LANES]
-                    out[w, at : at + rows, :] = piece.astype(f32)
+                    out[jnp.where(odd, wide - 1 - w, w), at : at + rows, :] = piece.astype(f32)
 
 
 def edge_body(dims, got, first, last):
@@ -293,6 +289,9 @@
     tiles = span // LANES
     per = thick * tiles * rows
     size_x = smear_e.shape[0]
+    w, n = lax.axis_index("wide"), lax.axis_index("narrow")
+    chunk = jnp.where(n % 2 == 1, wide - 1 - w, w)
+    own = n * wide + chunk
     for w in range(wide):
         entries[w : w + 1, :] = got[w, 2 * per : 2 * per + 1, :]
         for z in range(thick):
@@ -303,7 +302,7 @@
                 tp[to] = got[w, at : at + rows, :]
                 pp[to] = got[w, per + at : per + at + rows, :]
     for tx in range(span // size_x):
-        tile = (lax.axis_index("wide") * (span // size_x) + tx).astype(f32)
+        tile = (chunk * (span // size_x) + tx).astype(f32)
         hit = jnp.where(entries[...] == tile, expansion, 0.0)
         hit = jnp.max(hit, axis=1, keepdims=True)
         mask[:, tx * size_x : (tx + 1) * size_x] = jnp.broadcast_to(hit, (wide, size_x))
@@ -312,7 +311,6 @@
     mob_hi[...] = jnp.where(hi[depth:, :] > 0.5, mobility_liquid, mobility_vapor)
     r = lax.broadcasted_iota(jnp.int32, (rows, span), 0)
     c = lax.broadcasted_iota(jnp.int32, (rows, span), 1)
-    own = lax.axis_index("narrow") * wide + lax.axis_index("wide")
     no_lo, no_hi = own == 0, own == lax.axis_size("narrow") * wide - 1
 
     def at_z(z):
@@ -371,34 +369,97 @@
         total = total + parts[i]
     alpha = (rho[...] / jnp.sum(total, axis=1, keepdims=True))[:, :1]
     n = thick * rows
+    tiles = span // LANES
     for w in range(wide):
         at = slice(w * n, (w + 1) * n)
-        out[w, :n, :] = p[at, :] + alpha * d[at, :]
-        out[w, n : 2 * n, :] = r[at, :] - alpha * image[at, :]
-        if outer is not None:
-            out[w, 2 * n :, :] = outer[w]
-
-
-def spread_body(dims, got, *refs):
-    wide, thick, rows, span, _ = dims
-    inner, outs = (refs[0], refs[1:]) if len(refs) == 4 else (None, refs)
-    for k, out in enumerate(outs):
+        pressure = p[at, :] + alpha * d[at, :]
+        residual = r[at, :] - alpha * image[at, :]
+        if outer is None:
+            out[w, :n, :] = pressure
+            out[w, n : 2 * n, :] = residual
+            continue
+        units = [pressure[z * rows : (z + 1) * rows] for z in range(thick)]
+        units += [residual[z * rows : (z + 1) * rows] for z in (0, thick - 1)]
+        units += [outer[w, :rows, :], outer[w, rows:, :]]
+        for u, unit in enumerate(units):
+            for t in range(tiles):
+                to = (u * tiles + t) * rows
+                out[w, to : to + rows, :] = unit[:, t * LANES : (t + 1) * LANES]
+        to = len(units) * tiles * rows
+        for z in range(1, thick - 1):
+            for y in (z * rows, (z + 1) * rows - 1):
+                for t in range(tiles):
+                    out[w, to : to + 1, :] = residual[y : y + 1, t * LANES : (t + 1) * LANES]
+                    to += 1
+
+
+def spread_body(dims, got, pressure, residual):
+    wide, thick, rows, _, _ = dims
+    for k, out in enumerate((pressure, residual)):
         for z in range(thick):
             row = (k * thick + z) * rows
-            if k == 2:
-                if 0 < z < thick - 1:
-                    out[z] = inner[z - 1]
-                    continue
-                row = (2 * thick + (z > 0)) * rows
             for w in range(wide):
                 out[z, w * rows : (w + 1) * rows, :] = got[w, row : row + rows, :]
+
+
+def gather_body(dims, got, inner, source, mob, *refs):
+    wide, thick, rows, span, _ = dims
+    tiles = span // LANES
+    north = wide * rows
+    pressure, residual, heated = refs[3:6]
+    copies = [pltpu.make_async_copy(refs[3 + i], refs[i], refs[6].at[i]) for i in range(3)]
+    odd = lax.axis_index("narrow") % 2 == 1
+    planes = [(pressure, z) for z in range(thick)]
+    planes += [(out, z) for out in (residual, heated) for z in (0, thick - 1)]
+    for w in range(wide):
+        chunk = jnp.where(odd, wide - 1 - w, w)
+        y = pl.ds(pl.multiple_of(chunk * rows, rows), rows)
+        for u, (out, z) in enumerate(planes):
+            for t in range(tiles):
+                at = (u * tiles + t) * rows
+                out[z, y, t * LANES : (t + 1) * LANES] = got[w, at : at + rows, :]
+    for z in range(1, thick - 1):
+        heated[z] = inner[z - 1]
+    copies[0].start()
+    copies[2].start()
+    r = lax.broadcasted_iota(jnp.int32, (rows, span), 0)
+    c = lax.broadcasted_iota(jnp.int32, (rows, span), 1)
+    for z in range(1, thick - 1):
+
+        def part(i, z=z):
+            start = pl.multiple_of(i * rows, rows)
+            at = pl.ds(start, rows)
+            v, b = pressure[z, at, :], mob[z, at, :]
+            flux = jnp.where(c == span - 1, 0.0, (b + lane_roll(b, True)) * (v - lane_roll(v, True)))
+            total = flux - lane_roll(flux, False)
+            for k in (z - 1, z + 1):
+                total = total + (b + mob[k, at, :]) * (v - pressure[k, at, :])
+            y = jnp.minimum(start + rows, north - 1)
+            v_hi = jnp.where(r == rows - 1, pressure[z, pl.ds(y, 1), :], row_roll(v, True))
+            b_hi = jnp.where(r == rows - 1, mob[z, pl.ds(y, 1), :], row_roll(b, True))
+            y = jnp.maximum(start - 1, 0)
+            v_lo = jnp.where(r == 0, pressure[z, pl.ds(y, 1), :], row_roll(v, False))
+            b_lo = jnp.where(r == 0, mob[z, pl.ds(y, 1), :], row_roll(b, False))
+            total = total + (b + b_hi) * (v - v_hi) + (b + b_lo) * (v - v_lo)
+            residual[z, at, :] = source[z - 1, at, :] - (compress * v + 0.5 * total)
+
+        lax.fori_loop(0, wide, lambda i, carry: (part(i), carry)[1], 0)
+        first = len(planes) * tiles * rows + (z - 1) * 2 * tiles
+        for side, y in enumerate((0, north - 1)):
+            lower = 0 if side == 0 else wide - 1
+            w = jnp.where(odd, wide - 1 - lower, lower)
+            for t in range(tiles):
+                at = first + side * tiles + t
+                residual[z, y : y + 1, t * LANES : (t + 1) * LANES] = got[w, at : at + 1, :]
+    copies[1].start()
+    for copy in copies:
+        copy.wait()
 
 
 def forward_body(dims, tab, field, fold, spec, fwd, c_x, shift, message, extra):
     depth, rows, span = dims
     half = depth // 2
     size = half * rows
-    aligned = rows % 8 == 0
     for parity in range(2):
         for z in range(half):
             a = field[z * rows : (z + 1) * rows, :]
@@ -427,7 +488,7 @@
     forward_body(dims, tab, source, fold, spec, fwd, c_x, shift, message, jnp.zeros((1, LANES), f32))
 
 
-def solve_body(dims, tab, first_call, blocks, *refs):
+def solve_body(dims, tab, first_call, seats, *refs):
     depth, rows, span = dims
     half = depth // 2
     if first_call:
@@ -436,9 +497,10 @@
         (got, spec, shift, pairs, sine, wave, image_spec, h_old, rho,
          spec_new, h_new, message, alpha_out, low, high) = refs
     pair = pairs[lax.axis_index("narrow") * lax.axis_size("wide") + lax.axis_index("wide")]
-    for j in range(blocks):
-        low[j : j + 1, :] = got[j, 0:1, :span]
-        high[j : j + 1, :] = got[j, 0:1, span : 2 * span]
+    blocks = len(seats)
+    for j, i in enumerate(seats):
+        low[j : j + 1, :] = got[i, 0:1, :span]
+        high[j : j + 1, :] = got[i, 0:1, span : 2 * span]
     jump = high[...] - row_roll(low[...], True)
     r = lax.broadcasted_iota(jnp.int32, (blocks, span), 0)
     jump = jnp.where(r == blocks - 1, 0.0, jump)
@@ -468,10 +530,10 @@
                 acc = acc + e[i * 8 : (i + 1) * 8]
     total = total + fold_lanes(acc)
     zero = jnp.zeros((1, span), f32)
-    for j in range(blocks):
-        message[j, 0:1, :span] = zero if j == 0 else q[j - 1 : j]
-        message[j, 0:1, span : 2 * span] = q[j : j + 1]
-        message[j, 0:1, 2 * span :] = total
+    for j, i in enumerate(seats):
+        message[i, 0:1, :span] = zero if j == 0 else q[j - 1 : j]
+        message[i, 0:1, span : 2 * span] = q[j : j + 1]
+        message[i, 0:1, 2 * span :] = total
 
 
 def advance_body(dims, tab, first_call, last_call, blocks, *refs):
@@ -606,7 +668,7 @@
     most = listing.size
     heat_dims = (thick, north, span, size_y, size_x, most)
     heated, source = call(
-        lambda *r: heat_body(heat_dims, *r),
+        lambda *r: heat_body(heat_dims, False, *r),
         [(thick, north, span), (tiles_y, thick, size_y, span)],
         listing.reshape(-1), superheat_excess, liquid_indicator, zlo, zhi, ylo, yhi,
         smear_n, smear_e,
@@ -617,7 +679,6 @@
             VMEM((thick * north, span), f32),
             VMEM((tiles_y, span), f32),
         ],
-        name="heat",
     )
     source, mob = lax.optimization_barrier((source, mob))
     if size_y != rows:
@@ -629,7 +690,7 @@
     spec, message = call(
         lambda *r: start_body(dims[1], const["tab"], *r), [(whole, span), const["letter"]],
         source, const["forward"], const["c_x"], const["shift"],
-        scratch=[VMEM((whole, span), f32)], name="start",
+        scratch=[VMEM((whole, span), f32)],
     )
     return heated, source, mob.reshape(whole, span), mob_lo, mob_hi, spec, message
 
@@ -637,6 +698,7 @@
 def split_by_y(superheat_excess, liquid_indicator, listing, smear_n, smear_e, dims, const):
     depth, rows, span = dims[1]
     wide, thick = dims[0][:2]
+    lanes = lax.axis_size("narrow")
     whole = depth * rows
     per = thick * rows * (span // LANES)
     north = superheat_excess.shape[1]
@@ -650,20 +712,37 @@
             VMEM((8, LANES), f32),
             pltpu.SemaphoreType.DMA((2,)),
         ],
-        name="pack",
     )
     got = lax.all_to_all(packed, "wide", split_axis=0, concat_axis=0, tiled=True)
-    first, last = call(lambda *r: edge_body(dims[0], *r), [(2 * depth, span)] * 2, got, name="edge")
+    first, last = call(lambda *r: edge_body(dims[0], *r), [(2 * depth, span)] * 2, got)
     up, down = const["row_pairs"]
     lo = lax.ppermute(last, ("wide", "narrow"), up)
     hi = lax.ppermute(first, ("wide", "narrow"), down)
     full, plane = (whole, span), (depth, span)
-    return side_first, side_last, *call(
+    y_up = [(i, i + 1) for i in range(lanes - 1)]
+    y_down = [(i + 1, i) for i in range(lanes - 1)]
+    ylo = lax.ppermute(side_last, "narrow", y_up)
+    yhi = lax.ppermute(side_first, "narrow", y_down)
+    block, inner = (thick, north, span), (thick - 2, north, span)
+    size_y, size_x = smear_n.shape[0], smear_e.shape[0]
+    heat_dims = (thick, north, span, size_y, size_x, listing.size)
+    middle = call(
+        lambda *r: heat_body(heat_dims, True, *r),
+        [inner, inner, block],
+        listing.reshape(-1), superheat_excess, liquid_indicator, ylo, yhi, smear_n, smear_e,
+        smem=(0,),
+        scratch=[
+            VMEM(block, f32),
+            VMEM(((thick - 2) * north, span), f32),
+            VMEM((north // size_y, span), f32),
+        ],
+    )
+    lo, hi, *middle = lax.optimization_barrier((lo, hi, *middle))
+    return middle, *call(
         lambda *r: boil_body(dims[0], const["tab"], *r),
         [full, full, plane, plane, full, const["letter"], (wide, 2 * rows, span)],
         got, lo, hi, smear_n, smear_e, const["forward"], const["c_x"], const["shift"],
         scratch=[VMEM(full, f32)] * 4 + [VMEM((wide, span), f32), VMEM((wide, LANES), f32)],
-        name="boil",
     )
 
 
@@ -681,16 +760,23 @@
     full, one = (whole, span), (1, LANES)
     letter = (blocks, 1, 2 * span + LANES)
 
+    by_y = rows == size_y and thick > 2
+
+    def seat(j):
+        n, c = j // wide, j % wide
+        return n, wide - 1 - c if by_y and n % 2 == 1 else c
+
     def place(j):
-        return (j % wide) * lanes + j // wide
-
+        n, w = seat(j)
+        return w * lanes + n
+
+    seats = [n * wide + w for n, w in map(seat, range(blocks))]
     up = [(place(j), place(j + 1)) for j in range(blocks - 1)]
     const = {k: jnp.asarray(tab[k]) for k in ("c_x", "forward", "inverse", "swap", "shift", "pair", "sine", "wave")}
     const["tab"], const["letter"] = tab, letter
     const["row_pairs"] = up, [(b, a) for a, b in up]
-    by_y = rows == size_y and thick > 2
     if by_y:
-        side_first, side_last, source, mob, mob_lo, mob_hi, spec, message, outer = split_by_y(
+        middle, source, mob, mob_lo, mob_hi, spec, message, outer = split_by_y(
             superheat_excess, liquid_indicator, listing, smear_n, smear_e, dims, const
         )
     else:
@@ -704,9 +790,8 @@
     shift, pair, sine, wave = (const[k] for k in ("shift", "pair", "sine", "wave"))
     pair_scratch = [VMEM((blocks, span), f32)] * 2
     jump, message = call(
-        lambda *r: solve_body(shape, tab, True, blocks, *r), [(blocks, span), letter],
+        lambda *r: solve_body(shape, tab, True, seats, *r), [(blocks, span), letter],
         swap_all(message), spec, shift, pair, sine, wave, scratch=pair_scratch,
-        name="solve",
     )
     dir_spec = q = rho = None
     directions, images, alphas = [], [], []
@@ -725,7 +810,7 @@
             outs += [full, (2 * depth, span), full, letter]
         result = call(
             lambda *r, a=first, b=final: advance_body(shape, tab, a, b, blocks, *r), outs, *args,
-            scratch=work, name="advance",
+            scratch=work,
         )
         directions.append(result[0])
         images.append(result[1])
@@ -736,36 +821,33 @@
         else:
             dir_spec, q, image_spec, message = result[3:]
             spec, jump, message, alpha = call(
-                lambda *r: solve_body(shape, tab, False, blocks, *r),
+                lambda *r: solve_body(shape, tab, False, seats, *r),
                 [full, (blocks, span), letter, one],
                 swap_all(message), spec, shift, pair, sine, wave, image_spec, jump, rho,
-                scratch=pair_scratch, name="solve",
+                scratch=pair_scratch,
             )
             alphas.append(alpha)
 
-    extra = [outer] if by_y else []
+    if by_y:
+        extra = [outer]
+        tiles = span // LANES
+        lines = (thick + 4) * rows * tiles + -(-2 * (thick - 2) * tiles // 8) * 8
+        packet = (wide, lines, LANES)
+    else:
+        extra = []
+        packet = (wide, 2 * thick * rows, span)
     (both,) = call(
-        lambda *r: finish_body(dims[0], *r), [(wide, 2 * (thick + len(extra)) * rows, span)],
-        rho, parts, pressure, residual, directions[2], images[2], *extra, name="finish",
+        lambda *r: finish_body(dims[0], *r), [packet],
+        rho, parts, pressure, residual, directions[2], images[2], *extra,
     )
     both = lax.all_to_all(both, "wide", split_axis=0, concat_axis=0, tiled=True)
-    outs = [(thick, north, span)] * (2 + len(extra))
+    block = (thick, north, span)
     if not by_y:
-        pressure, residual = call(
-            lambda *r: spread_body(dims[0], *r), outs, both, name="spread"
-        )
+        pressure, residual = call(lambda *r: spread_body(dims[0], *r), [block] * 2, both)
         return heated, pressure, residual
-    y_up = [(i, i + 1) for i in range(lanes - 1)]
-    y_down = [(i + 1, i) for i in range(lanes - 1)]
-    ylo = lax.ppermute(side_last, "narrow", y_up)
-    yhi = lax.ppermute(side_first, "narrow", y_down)
-    (inner,) = call(
-        lambda *r: heat_body((thick, north, span, size_y, span, 0), *r),
-        [(thick - 2, north, span)], superheat_excess, liquid_indicator, ylo, yhi,
-        scratch=[VMEM((thick, north, span), f32)], name="heat",
-    )
     pressure, residual, heated = call(
-        lambda *r: spread_body(dims[0], *r), outs, both, inner, name="spread"
+        lambda *r: gather_body(dims[0], *r), [block] * 3, both, *middle, far_out=True,
+        scratch=[VMEM(block, f32)] * 3 + [pltpu.SemaphoreType.DMA((3,))],
     )
     return heated, pressure, residual
 

time: 250 us -> 243 us (0.972)
  waiting for transfers between devices: 59 us -> 3.01 us
  blocking collectives: 133 us -> 184 us
  Pallas kernels: 39.9 us -> 42.7 us
    all_to_all x0 -> x1, blocking collectives: none -> 52.9 us  [on_device(): both = lax.all_to_all(both, 'wide', split_axis=0, concat_axis=0, tiled=True)]
    all_to_all x1 -> x0, waiting for transfers between devices: 51 us -> none  [on_device(): both = lax.all_to_all(both, 'wide', split_axis=0, concat_axis=0, tiled=True)]
    ppermute x1, waiting for transfers between devices: 4.68 us -> 0.01 us  [split_by_y(): hi = lax.ppermute(first, ('wide', 'narrow'), down)]
    all_to_all x1 -> x0, starting transfers between devices: 3.63 us -> none  [on_device(): both = lax.all_to_all(both, 'wide', split_axis=0, concat_axis=0, tiled=True)]
    pallas_call x12, Pallas kernels: 39.9 us -> 42.7 us  [call(): pl.pallas_call(body, out_shape=[jax.ShapeDtypeStruct(s, f32) for s in out...]
    all_to_all x7, blocking collectives: 76.6 us -> 74 us  [swap_all(): return lax.all_to_all(x, ORDER, split_axis=0, concat_axis=0, tiled=True)]
    unnamed x30 -> x26, local copies, waits for them, and re-layouts: 5.6 us -> 3.16 us
  transfers between devices with their start and end apart: 5 -> 4, of which waited for: 4 -> 1; matrix products, arithmetic and copies ran while one was open for 0% -> 0% of each run, Pallas kernels for 0% -> 1%
where the time goes in v3:
time: 243 us; the launch traced here: 242 us
  blocking collectives  184 us (76%)
  Pallas kernels  42.7 us (18%)
  starting transfers between devices  8.76 us (4%)
  local copies, waits for them, and re-layouts  3.16 us (1%)
  waiting for transfers between devices  3.01 us (1%)
    all_to_all x7, blocking collectives, swap_all(): return lax.all_to_all(x, ORDER, split_axis=0, concat_axis=0, tiled=True)  74 us
    all_to_all x1, blocking collectives, split_by_y(): lax.all_to_all(packed, 'wide', split_axis=0, concat_axis=0, tiled=True)  56.8 us
    all_to_all x1, blocking collectives, on_device(): both = lax.all_to_all(both, 'wide', split_axis=0, concat_axis=0, tiled=True)  52.9 us
    pallas_call x12, Pallas kernels, call(): pl.pallas_call(body, out_shape=[jax.ShapeDtypeStruct(s, f32) for s in out...  42.7 us
  transfers between devices with their start and end apart: 4, of which 1 were waited for; matrix products, arithmetic and copies ran while one was open for 0% of the time, Pallas kernels for 1%

profile of v3, /device:TPU:0, one launch (start us, length us, event | category | flops | bytes accessed | tf_op | source)
XLA Modules:
  0.0 242.4 jit_solution(5085983458044778179)
XLA Ops:
  0.6 1.2 copy-done.7
  1.9 1.2 copy-done.8
  3.1 0.7 copy-done.9
  3.7 0.3 shard_map.148
  4.1 56.8 %all_to_all.45.r_0_ = f32[8,520,128]{2,1,0:T(8,128)S(1)} all-to-all(f32[8,520,128]{2,1,0:T(8,128)S(1)} %get-tuple-element.55), channel_id=1, replica_groups=mesh['wide'=8,'narrow'=4] {'wide'}, dimensions={0} | all-to-all | bytes 4259840 | tf_op jit(solution)/shard_map/all_to_all | solution.py:716
  60.8 0.2 shard_map.149
  61.0 0.0 copy-start
  61.0 0.0 copy-start.1
  61.0 0.0 copy-start.3
  61.1 2.7 %collective-permute-start = (f32[64,512]{1,0:T(8,128)S(1)}, f32[64,512]{1,0:T(8,128)S(1)}, u32[]{:S(2)}, u32[]{:S(2)}) collective-permute-start(f32[64,512]{1,0:T(8,128)S(1)} %get-tuple-element.56), channel_id=1, source_target_pairs={{0,4},{4,8},{8,12},{12,16},{16,20},{20,24},{24,28},{28,29},{29,25}... | collective-permute-start | bytes 393224 | tf_op jit(solution)/shard_map/ppermute | solution.py:719
  63.8 1.3 collective-permute-start.1
  65.1 3.4 %collective-permute-start.2 = (f32[2,4,1,512]{3,2,1,0:T(1,128)S(1)}, f32[2,4,1,512]{3,2,1,0:T(1,128)S(1)}, u32[]{:S(2)}, u32[]{:S(2)}) collective-permute-start(f32[2,4,1,512]{3,2,1,0:T(1,128)S(1)} %get-tuple-element.58), channel_id=1, source_target_pairs={{0,1},{1,2},{2,3},{4,5},{5,6},{6,7},{8,9},{9,10},{10,11},{12,13},{... | collective-permute-start | bytes 49160 | tf_op jit(solution)/shard_map/ppermute | solution.py:724
  68.5 1.3 collective-permute-start.3
  69.9 3.0 %collective-permute-done.3.r_4_ = f32[2,4,1,512]{3,2,1,0:T(1,128)S(1)} collective-permute-done((f32[2,4,1,512]{3,2,1,0:T(1,128)S(1)}, f32[2,4,1,512]{3,2,1,0:T(1,128)S(1)}, u32[]{:S(2)}, u32[]{:S(2)}) %collective-permute-start.3) | collective-permute-done | bytes 16416 | tf_op jit(solution)/shard_map/ppermute | solution.py:725
  72.9 3.3 %shard_map.150 = (f32[2,128,512]{2,1,0:T(8,128)S(1)}, f32[2,128,512]{2,1,0:T(8,128)S(1)}, f32[4,128,512]{2,1,0:T(8,128)S(1)}) custom-call(s32[16]{0:T(128)S(1)} %bitcast.1, f32[4,128,512]{2,1,0:T(8,128)S(1)} %copy-done.7, s32[4,128,512]{2,1,0:T(8,128)S(1)} %copy-done.8, f32[2,4,1,512]{3,2,1,0:T(1,128)S(1)} %collective-permute-done.2.r_3_, ...), custom_call_target="tpu_custom_call" | custom-call | flops 1000000000 | bytes 4194304 | tf_op jit(solution)/shard_map/pallas_call | solution.py:98
  76.3 9.3 %shard_map.151 = (f32[512,512]{1,0:T(8,128)S(1)}, f32[512,512]{1,0:T(8,128)S(1)}, f32[32,512]{1,0:T(8,128)S(1)}, f32[32,512]{1,0:T(8,128)S(1)}, f32[512,512]{1,0...) custom-call(f32[8,520,128]{2,1,0:T(8,128)S(1)} %all_to_all.45.r_0_, ...), custom_call_target="tpu_custom_call" | custom-call | flops 1000000000 | bytes 4194304 | tf_op jit(solution)/shard_map/pallas_call | solution.py:98
  85.6 12.8 %all_to_all.46.r_0_ = f32[32,1,1152]{2,1,0:T(1,128)S(1)} all-to-all(f32[32,1,1152]{2,1,0:T(1,128)S(1)} %get-tuple-element.65), channel_id=1, replica_groups=mesh['wide'=8,'narrow'=4] {'narrow','wide'}, dimensions={0} | all-to-all | bytes 294912 | tf_op jit(solution)/shard_map/all_to_all | solution.py:788
  98.4 0.5 shard_map.152
  98.9 10.3 %all_to_all.47.r_0_ = f32[32,1,1152]{2,1,0:T(1,128)S(1)} all-to-all(f32[32,1,1152]{2,1,0:T(1,128)S(1)} %get-tuple-element.67), channel_id=1, replica_groups=mesh['wide'=8,'narrow'=4] {'narrow','wide'}, dimensions={0} | all-to-all | bytes 294912 | tf_op jit(solution)/shard_map/all_to_all | solution.py:788
  109.2 8.5 %shard_map.153 = (f32[512,512]{1,0:T(8,128)S(1)}, f32[512,512]{1,0:T(8,128)S(1)}, f32[1,128]{1,0:T(1,128)S(1)}, f32[512,512]{1,0:T(8,128)S(1)}, f32[64,512]{1,0:...) custom-call(f32[32,1,1152]{2,1,0:T(1,128)S(1)} %all_to_all.47.r_0_, ...), custom_call_target="tpu_custom_call" | custom-call | flops 1000000000 | bytes 4194304 | tf_op jit(solution)/shard_map/pallas_call | solution.py:98
  117.7 10.3 %all_to_all.48.r_0_ = f32[32,1,1152]{2,1,0:T(1,128)S(1)} all-to-all(f32[32,1,1152]{2,1,0:T(1,128)S(1)} %get-tuple-element.71), channel_id=1, replica_groups=mesh['wide'=8,'narrow'=4] {'narrow','wide'}, dimensions={0} | all-to-all | bytes 294912 | tf_op jit(solution)/shard_map/all_to_all | solution.py:788
  128.0 0.6 shard_map.154
  128.6 10.3 %all_to_all.49.r_0_ = f32[32,1,1152]{2,1,0:T(1,128)S(1)} all-to-all(f32[32,1,1152]{2,1,0:T(1,128)S(1)} %get-tuple-element.75), channel_id=1, replica_groups=mesh['wide'=8,'narrow'=4] {'narrow','wide'}, dimensions={0} | all-to-all | bytes 294912 | tf_op jit(solution)/shard_map/all_to_all | solution.py:788
  139.0 8.5 %shard_map.155 = (f32[512,512]{1,0:T(8,128)S(1)}, f32[512,512]{1,0:T(8,128)S(1)}, f32[1,128]{1,0:T(1,128)S(1)}, f32[512,512]{1,0:T(8,128)S(1)}, f32[64,512]{1,0:...) custom-call(f32[32,1,1152]{2,1,0:T(1,128)S(1)} %all_to_all.49.r_0_, ...), custom_call_target="tpu_custom_call" | custom-call | flops 1000000000 | bytes 4194304 | tf_op jit(solution)/shard_map/pallas_call | solution.py:98
  147.5 10.3 %all_to_all.50.r_0_ = f32[32,1,1152]{2,1,0:T(1,128)S(1)} all-to-all(f32[32,1,1152]{2,1,0:T(1,128)S(1)} %get-tuple-element.79), channel_id=1, replica_groups=mesh['wide'=8,'narrow'=4] {'narrow','wide'}, dimensions={0} | all-to-all | bytes 294912 | tf_op jit(solution)/shard_map/all_to_all | solution.py:788
  157.8 1.1 shard_map.156
  158.9 10.3 %all_to_all.51.r_0_ = f32[32,1,1152]{2,1,0:T(1,128)S(1)} all-to-all(f32[32,1,1152]{2,1,0:T(1,128)S(1)} %get-tuple-element.83), channel_id=1, replica_groups=mesh['wide'=8,'narrow'=4] {'narrow','wide'}, dimensions={0} | all-to-all | bytes 294912 | tf_op jit(solution)/shard_map/all_to_all | solution.py:788
  169.3 6.1 %shard_map.157 = (f32[512,512]{1,0:T(8,128)S(1)}, f32[512,512]{1,0:T(8,128)S(1)}, f32[1,128]{1,0:T(1,128)S(1)}, f32[32,1,128]{2,1,0:T(1,128)S(1)}, f32[512,512]{1,0:T(8,128)S(1)}, /*index=5*/f32[512,512]{1,0:T(8,128)S(1)}) custom-call(f32[32,1,1152]{2,1,0:T(1,128)S(1)} %all_to_all.51.r_0_, f32[512,512]{1,0:T(8,128)S(1)} %get-tuple-element.84.r_1_, ...), custom_call_target="tpu_custom_call" | custom-call | flops 1000000000 | bytes 4194304 | tf_op jit(solution)/shard_map/pallas_call | solution.py:98
  175.3 9.6 %all_to_all.52.r_1_ = f32[32,1,128]{2,1,0:T(1,128)S(1)} all-to-all(f32[32,1,128]{2,1,0:T(1,128)S(1)} %get-tuple-element.95), channel_id=1, replica_groups=mesh['wide'=8,'narrow'=4] {'narrow','wide'}, dimensions={0} | all-to-all | bytes 32768 | tf_op jit(solution)/shard_map/all_to_all | solution.py:788
  184.9 0.4 shard_map.158
  185.4 52.9 %all_to_all.53.r_0_ = f32[8,528,128]{2,1,0:T(8,128)S(1)} all-to-all(f32[8,528,128]{2,1,0:T(8,128)S(1)} %shard_map.158), channel_id=1, replica_groups=mesh['wide'=8,'narrow'=4] {'wide'}, dimensions={0} | all-to-all | bytes 4325376 | tf_op jit(solution)/shard_map/all_to_all | solution.py:843
  238.3 3.9 %shard_map.159 = (f32[4,128,512]{2,1,0:T(8,128)}, f32[4,128,512]{2,1,0:T(8,128)}, f32[4,128,512]{2,1,0:T(8,128)}) custom-call(f32[8,528,128]{2,1,0:T(8,128)S(1)} %all_to_all.53.r_0_, f32[2,128,512]{2,1,0:T(8,128)S(1)} %get-tuple-element.101.r_1_, f32[2,128,512]{2,1,0:T(8,128)S(1)} %get-tuple-element.102.r_2_, f32[4,128,512]{2,1,0:T(8,128)S(1)} %get-tuple-element.103.r_3_), custom_call_target="tpu_custom_call" | custom-call | flops 1000000000 | bytes 4194304 | tf_op jit(solution)/shard_map/pallas_call | solution.py:98
  (23 shorter events, 0.1 us)
Async XLA Ops:
  0.6 1.2 copy-start.7
  1.9 1.2 copy-start.8
  3.1 0.7 copy-start.9
  60.8 12.0 %copy-start.5 = (f32[128,128]{1,0:T(8,128)S(1)}, f32[128,128]{1,0:T(8,128)}, u32[]{:S(2)}) copy-start(f32[128,128]{1,0:T(8,128)} %r_4_.7) | copy-start | bytes 196612
  60.8 12.0 %copy-start.6 = (f32[16,16]{1,0:T(8,128)S(1)}, f32[16,16]{1,0:T(8,128)}, u32[]{:S(2)}) copy-start(f32[16,16]{1,0:T(8,128)} %r_3_.7) | copy-start | bytes 3076
  61.0 15.2 %copy-start = (f32[512,512]{1,0:T(8,128)S(1)}, f32[512,512]{1,0:T(8,128)}, u32[]{:S(2)}) copy-start(f32[512,512]{1,0:T(8,128)} %constant.16.clone.r_6_.r_5_) | copy-start | bytes 3145732
  61.0 15.2 %copy-start.1 = (f32[2,256,256]{2,1,0:T(8,128)S(1)}, f32[2,256,256]{2,1,0:T(8,128)}, u32[]{:S(2)}) copy-start(f32[2,256,256]{2,1,0:T(8,128)} %constant.17.clone.r_5_.r_4_) | copy-start | bytes 1572868
  61.0 15.2 %copy-start.3 = (f32[32,512]{1,0:T(8,128)S(1)}, f32[32,512]{1,0:T(8,128)}, u32[]{:S(2)}) copy-start(f32[32,512]{1,0:T(8,128)} %constant.20.clone.r_7_.r_2_) | copy-start | bytes 196612
  61.1 15.1 %collective-permute-start = (f32[64,512]{1,0:T(8,128)S(1)}, f32[64,512]{1,0:T(8,128)S(1)}, u32[]{:S(2)}, u32[]{:S(2)}) collective-permute-start(f32[64,512]{1,0:T(8,128)S(1)} %get-tuple-element.56), channel_id=1, source_target_pairs={{0,4},{4,8},{8,12},{12,16},{16,20},{20,24},{24,28},{28,29},{29,25}... | collective-permute-start | bytes 393224 | tf_op jit(solution)/shard_map/ppermute | solution.py:719
  63.8 12.4 %collective-permute-start.1 = (f32[64,512]{1,0:T(8,128)S(1)}, f32[64,512]{1,0:T(8,128)S(1)}, u32[]{:S(2)}, u32[]{:S(2)}) collective-permute-start(f32[64,512]{1,0:T(8,128)S(1)} %get-tuple-element.57), channel_id=1, source_target_pairs={{4,0},{8,4},{12,8},{16,12},{20,16},{24,20},{28,24},{29,28},{25,29}... | collective-permute-start | bytes 393224 | tf_op jit(solution)/shard_map/ppermute | solution.py:720
  65.1 4.8 %collective-permute-start.2 = (f32[2,4,1,512]{3,2,1,0:T(1,128)S(1)}, f32[2,4,1,512]{3,2,1,0:T(1,128)S(1)}, u32[]{:S(2)}, u32[]{:S(2)}) collective-permute-start(f32[2,4,1,512]{3,2,1,0:T(1,128)S(1)} %get-tuple-element.58), channel_id=1, source_target_pairs={{0,1},{1,2},{2,3},{4,5},{5,6},{6,7},{8,9},{9,10},{10,11},{12,13},{... | collective-permute-start | bytes 49160 | tf_op jit(solution)/shard_map/ppermute | solution.py:724
  68.5 4.3 %collective-permute-start.3 = (f32[2,4,1,512]{3,2,1,0:T(1,128)S(1)}, f32[2,4,1,512]{3,2,1,0:T(1,128)S(1)}, u32[]{:S(2)}, u32[]{:S(2)}) collective-permute-start(f32[2,4,1,512]{3,2,1,0:T(1,128)S(1)} %get-tuple-element.59), channel_id=1, source_target_pairs={{1,0},{2,1},{3,2},{5,4},{6,5},{7,6},{9,8},{10,9},{11,10},{13,12},{... | collective-permute-start | bytes 49160 | tf_op jit(solution)/shard_map/ppermute | solution.py:725
  76.2 22.1 %copy-start.10 = (f32[32,2,512]{2,1,0:T(2,128)S(1)}, f32[32,2,512]{2,1,0:T(2,128)}, u32[]{:S(2)}) copy-start(f32[32,2,512]{2,1,0:T(2,128)} %constant.21.clone.r_3_) | copy-start | bytes 393220
  76.2 22.1 %copy-start.11 = (f32[32,128]{1,0:T(8,128)S(1)}, f32[32,128]{1,0:T(8,128)}, u32[]{:S(2)}) copy-start(f32[32,128]{1,0:T(8,128)} %constant.23.clone.r_5_) | copy-start | bytes 49156
  76.2 22.1 %copy-start.12 = (f32[32,32]{1,0:T(8,128)S(1)}, f32[32,32]{1,0:T(8,128)}, u32[]{:S(2)}) copy-start(f32[32,32]{1,0:T(8,128)} %constant.22.clone.r_4_) | copy-start | bytes 12292
  85.5 23.7 %copy-start.2 = (f32[2,256,256]{2,1,0:T(8,128)S(1)}, f32[2,256,256]{2,1,0:T(8,128)}, u32[]{:S(2)}) copy-start(f32[2,256,256]{2,1,0:T(8,128)} %constant.18.clone.r_3_) | copy-start | bytes 1572868
  85.5 23.6 %copy-start.4 = (f32[64,64]{1,0:T(8,128)S(1)}, f32[64,64]{1,0:T(8,128)}, u32[]{:S(2)}) copy-start(f32[64,64]{1,0:T(8,128)} %constant.19.clone.r_6_) | copy-start | bytes 49156

commit v4 on v3

--- a/solution.py
+++ b/solution.py
@@ -267,7 +267,13 @@
                     out[jnp.where(odd, wide - 1 - w, w), at : at + rows, :] = piece.astype(f32)
 
 
-def edge_body(dims, got, first, last):
+def edge_body(dims, lam, got, shift, first, last, scale):
+    half = shift.shape[0] // 2
+    for parity in range(2):
+        mu = shift[parity * half : (parity + 1) * half, :]
+        for ky, value in enumerate(lam):
+            at = (parity * len(lam) + ky) * half
+            scale[at : at + half, :] = 1.0 / (mu + value)
     wide, thick, rows, span, _ = dims
     tiles = span // LANES
     per = thick * tiles * rows
@@ -469,12 +475,11 @@
             mat(fwd[parity], fold[:size, :]), c_x[...]
         )
     for parity in range(2):
-        mu = shift[parity * half : (parity + 1) * half, :]
         low = jnp.zeros((half, span), f32)
         high = jnp.zeros((half, span), f32)
         for ky in range(rows):
             at = parity * size + ky * half
-            g = spec[at : at + half, :] / (mu + tab["lam"][ky])
+            g = spec[at : at + half, :] * shift[at : at + half, :]
             low = low + tab["first"][ky] * g
             high = high + tab["last"][ky] * g
         for k in range(half):
@@ -488,7 +493,7 @@
     forward_body(dims, tab, source, fold, spec, fwd, c_x, shift, message, jnp.zeros((1, LANES), f32))
 
 
-def solve_body(dims, tab, first_call, seats, *refs):
+def solve_body(dims, first_call, seats, *refs):
     depth, rows, span = dims
     half = depth // 2
     if first_call:
@@ -518,14 +523,13 @@
     total = fold_lanes(q * jump) * -1.0
     acc = jnp.zeros((8, span), f32)
     for parity in range(2):
-        mu = shift[parity * half : (parity + 1) * half, :]
         for ky in range(rows):
             at = parity * half * rows + ky * half
             s = spec[at : at + half, :]
             if not first_call:
                 s = s - alpha * image_spec[at : at + half, :]
                 spec_new[at : at + half, :] = s
-            e = s * s / (mu + tab["lam"][ky])
+            e = s * s * shift[at : at + half, :]
             for i in range(half // 8):
                 acc = acc + e[i * 8 : (i + 1) * 8]
     total = total + fold_lanes(acc)
@@ -571,13 +575,12 @@
         beta = (rho / rho_old[...])[:, :1]
     for parity in range(2):
         at_q = parity * half
-        mu = shift[at_q : at_q + half, :]
         q_lo = q_mid[at_q : at_q + half, :]
         q_hi = q_mid[depth + at_q : depth + at_q + half, :]
         for ky in range(rows):
             at = parity * size + ky * half
-            u = (spec[at : at + half, :] + tab["first"][ky] * q_lo - tab["last"][ky] * q_hi) / (
-                mu + tab["lam"][ky]
+            u = (spec[at : at + half, :] + tab["first"][ky] * q_lo - tab["last"][ky] * q_hi) * (
+                shift[at : at + half, :]
             )
             if not first_call:
                 u = u + beta * dir_old[at : at + half, :]
@@ -714,7 +717,10 @@
         ],
     )
     got = lax.all_to_all(packed, "wide", split_axis=0, concat_axis=0, tiled=True)
-    first, last = call(lambda *r: edge_body(dims[0], *r), [(2 * depth, span)] * 2, got)
+    first, last, const["shift"] = call(
+        lambda *r: edge_body(dims[0], const["tab"]["lam"], *r),
+        [(2 * depth, span)] * 2 + [(whole, span)], got, const["shift"],
+    )
     up, down = const["row_pairs"]
     lo = lax.ppermute(last, ("wide", "narrow"), up)
     hi = lax.ppermute(first, ("wide", "narrow"), down)
@@ -775,6 +781,10 @@
     const = {k: jnp.asarray(tab[k]) for k in ("c_x", "forward", "inverse", "swap", "shift", "pair", "sine", "wave")}
     const["tab"], const["letter"] = tab, letter
     const["row_pairs"] = up, [(b, a) for a, b in up]
+    if not by_y:
+        mu = const["shift"].reshape(2, 1, depth // 2, span)
+        lam = jnp.asarray(tab["lam"], f32).reshape(1, rows, 1, 1)
+        const["shift"] = (1.0 / (mu + lam)).reshape(full)
     if by_y:
         middle, source, mob, mob_lo, mob_hi, spec, message, outer = split_by_y(
             superheat_excess, liquid_indicator, listing, smear_n, smear_e, dims, const
@@ -790,7 +800,7 @@
     shift, pair, sine, wave = (const[k] for k in ("shift", "pair", "sine", "wave"))
     pair_scratch = [VMEM((blocks, span), f32)] * 2
     jump, message = call(
-        lambda *r: solve_body(shape, tab, True, seats, *r), [(blocks, span), letter],
+        lambda *r: solve_body(shape, True, seats, *r), [(blocks, span), letter],
         swap_all(message), spec, shift, pair, sine, wave, scratch=pair_scratch,
     )
     dir_spec = q = rho = None
@@ -821,7 +831,7 @@
         else:
             dir_spec, q, image_spec, message = result[3:]
             spec, jump, message, alpha = call(
-                lambda *r: solve_body(shape, tab, False, seats, *r),
+                lambda *r: solve_body(shape, False, seats, *r),
                 [full, (blocks, span), letter, one],
                 swap_all(message), spec, shift, pair, sine, wave, image_spec, jump, rho,
                 scratch=pair_scratch,

time: 243 us -> 243 us (level)
  no operation moved by 1% of the time
where the time goes in v4:
time: 243 us; the launch traced here: 242 us
  blocking collectives  184 us (76%)
  Pallas kernels  42.7 us (18%)
  starting transfers between devices  8.76 us (4%)
  local copies, waits for them, and re-layouts  3.16 us (1%)
  waiting for transfers between devices  3.01 us (1%)
    all_to_all x7, blocking collectives, swap_all(): return lax.all_to_all(x, ORDER, split_axis=0, concat_axis=0, tiled=True)  74 us
    all_to_all x1, blocking collectives, split_by_y(): lax.all_to_all(packed, 'wide', split_axis=0, concat_axis=0, tiled=True)  56.9 us
    all_to_all x1, blocking collectives, on_device(): both = lax.all_to_all(both, 'wide', split_axis=0, concat_axis=0, tiled=True)  52.9 us
    pallas_call x12, Pallas kernels, call(): pl.pallas_call(body, out_shape=[jax.ShapeDtypeStruct(s, f32) for s in out...  42.7 us
  transfers between devices with their start and end apart: 4, of which 1 were waited for; matrix products, arithmetic and copies ran while one was open for 0% of the time, Pallas kernels for 1%

profile of v4, /device:TPU:0, one launch (start us, length us, event | category | flops | bytes accessed | tf_op | source)
XLA Modules:
  0.0 242.5 jit_solution(9383691723740069421)
XLA Ops:
  0.6 1.2 copy-done.6
  1.9 1.2 copy-done.7
  3.1 0.7 copy-done.8
  3.7 0.3 shard_map.148
  4.1 0.0 copy-start.10
  4.1 56.9 %all_to_all.45.r_0_ = f32[8,520,128]{2,1,0:T(8,128)S(1)} all-to-all(f32[8,520,128]{2,1,0:T(8,128)S(1)} %get-tuple-element.56), channel_id=1, replica_groups=mesh['wide'=8,'narrow'=4] {'wide'}, dimensions={0} | all-to-all | bytes 4259840 | tf_op jit(solution)/shard_map/all_to_all | solution.py:719
  61.0 0.3 shard_map.149
  61.3 0.0 copy-start
  61.3 2.7 %collective-permute-start = (f32[64,512]{1,0:T(8,128)S(1)}, f32[64,512]{1,0:T(8,128)S(1)}, u32[]{:S(2)}, u32[]{:S(2)}) collective-permute-start(f32[64,512]{1,0:T(8,128)S(1)} %get-tuple-element.57), channel_id=1, source_target_pairs={{0,4},{4,8},{8,12},{12,16},{16,20},{20,24},{24,28},{28,29},{29,25}... | collective-permute-start | bytes 393224 | tf_op jit(solution)/shard_map/ppermute | solution.py:725
  64.0 1.3 collective-permute-start.1
  65.3 3.4 %collective-permute-start.2 = (f32[2,4,1,512]{3,2,1,0:T(1,128)S(1)}, f32[2,4,1,512]{3,2,1,0:T(1,128)S(1)}, u32[]{:S(2)}, u32[]{:S(2)}) collective-permute-start(f32[2,4,1,512]{3,2,1,0:T(1,128)S(1)} %get-tuple-element.59), channel_id=1, source_target_pairs={{0,1},{1,2},{2,3},{4,5},{5,6},{6,7},{8,9},{9,10},{10,11},{12,13},{... | collective-permute-start | bytes 49160 | tf_op jit(solution)/shard_map/ppermute | solution.py:730
  68.8 1.3 collective-permute-start.3
  70.1 3.0 %collective-permute-done.3.r_4_ = f32[2,4,1,512]{3,2,1,0:T(1,128)S(1)} collective-permute-done((f32[2,4,1,512]{3,2,1,0:T(1,128)S(1)}, f32[2,4,1,512]{3,2,1,0:T(1,128)S(1)}, u32[]{:S(2)}, u32[]{:S(2)}) %collective-permute-start.3) | collective-permute-done | bytes 16416 | tf_op jit(solution)/shard_map/ppermute | solution.py:731
  73.1 3.3 %shard_map.150 = (f32[2,128,512]{2,1,0:T(8,128)S(1)}, f32[2,128,512]{2,1,0:T(8,128)S(1)}, f32[4,128,512]{2,1,0:T(8,128)S(1)}) custom-call(s32[16]{0:T(128)S(1)} %bitcast.1, f32[4,128,512]{2,1,0:T(8,128)S(1)} %copy-done.6, s32[4,128,512]{2,1,0:T(8,128)S(1)} %copy-done.7, f32[2,4,1,512]{3,2,1,0:T(1,128)S(1)} %collective-permute-done.2.r_3_, ...), custom_call_target="tpu_custom_call" | custom-call | flops 1000000000 | bytes 4194304 | tf_op jit(solution)/shard_map/pallas_call | solution.py:98
  76.4 0.0 copy-start.9
  76.5 9.3 %shard_map.151 = (f32[512,512]{1,0:T(8,128)S(1)}, f32[512,512]{1,0:T(8,128)S(1)}, f32[32,512]{1,0:T(8,128)S(1)}, f32[32,512]{1,0:T(8,128)S(1)}, f32[512,512]{1,0...) custom-call(f32[8,520,128]{2,1,0:T(8,128)S(1)} %all_to_all.45.r_0_, ...), custom_call_target="tpu_custom_call" | custom-call | flops 1000000000 | bytes 4194304 | tf_op jit(solution)/shard_map/pallas_call | solution.py:98
  85.8 12.8 %all_to_all.46.r_0_ = f32[32,1,1152]{2,1,0:T(1,128)S(1)} all-to-all(f32[32,1,1152]{2,1,0:T(1,128)S(1)} %get-tuple-element.67), channel_id=1, replica_groups=mesh['wide'=8,'narrow'=4] {'narrow','wide'}, dimensions={0} | all-to-all | bytes 294912 | tf_op jit(solution)/shard_map/all_to_all | solution.py:798
  98.6 0.4 shard_map.152
  99.0 10.3 %all_to_all.47.r_0_ = f32[32,1,1152]{2,1,0:T(1,128)S(1)} all-to-all(f32[32,1,1152]{2,1,0:T(1,128)S(1)} %get-tuple-element.69), channel_id=1, replica_groups=mesh['wide'=8,'narrow'=4] {'narrow','wide'}, dimensions={0} | all-to-all | bytes 294912 | tf_op jit(solution)/shard_map/all_to_all | solution.py:798
  109.3 8.4 %shard_map.153 = (f32[512,512]{1,0:T(8,128)S(1)}, f32[512,512]{1,0:T(8,128)S(1)}, f32[1,128]{1,0:T(1,128)S(1)}, f32[512,512]{1,0:T(8,128)S(1)}, f32[64,512]{1,0:...) custom-call(f32[32,1,1152]{2,1,0:T(1,128)S(1)} %all_to_all.47.r_0_, ...), custom_call_target="tpu_custom_call" | custom-call | flops 1000000000 | bytes 4194304 | tf_op jit(solution)/shard_map/pallas_call | solution.py:98
  117.8 10.3 %all_to_all.48.r_0_ = f32[32,1,1152]{2,1,0:T(1,128)S(1)} all-to-all(f32[32,1,1152]{2,1,0:T(1,128)S(1)} %get-tuple-element.73), channel_id=1, replica_groups=mesh['wide'=8,'narrow'=4] {'narrow','wide'}, dimensions={0} | all-to-all | bytes 294912 | tf_op jit(solution)/shard_map/all_to_all | solution.py:798
  128.1 0.6 shard_map.154
  128.7 10.3 %all_to_all.49.r_0_ = f32[32,1,1152]{2,1,0:T(1,128)S(1)} all-to-all(f32[32,1,1152]{2,1,0:T(1,128)S(1)} %get-tuple-element.77), channel_id=1, replica_groups=mesh['wide'=8,'narrow'=4] {'narrow','wide'}, dimensions={0} | all-to-all | bytes 294912 | tf_op jit(solution)/shard_map/all_to_all | solution.py:798
  139.0 8.5 %shard_map.155 = (f32[512,512]{1,0:T(8,128)S(1)}, f32[512,512]{1,0:T(8,128)S(1)}, f32[1,128]{1,0:T(1,128)S(1)}, f32[512,512]{1,0:T(8,128)S(1)}, f32[64,512]{1,0:...) custom-call(f32[32,1,1152]{2,1,0:T(1,128)S(1)} %all_to_all.49.r_0_, ...), custom_call_target="tpu_custom_call" | custom-call | flops 1000000000 | bytes 4194304 | tf_op jit(solution)/shard_map/pallas_call | solution.py:98
  147.6 10.3 %all_to_all.50.r_0_ = f32[32,1,1152]{2,1,0:T(1,128)S(1)} all-to-all(f32[32,1,1152]{2,1,0:T(1,128)S(1)} %get-tuple-element.81), channel_id=1, replica_groups=mesh['wide'=8,'narrow'=4] {'narrow','wide'}, dimensions={0} | all-to-all | bytes 294912 | tf_op jit(solution)/shard_map/all_to_all | solution.py:798
  157.9 1.1 shard_map.156
  159.0 10.3 %all_to_all.51.r_0_ = f32[32,1,1152]{2,1,0:T(1,128)S(1)} all-to-all(f32[32,1,1152]{2,1,0:T(1,128)S(1)} %get-tuple-element.85), channel_id=1, replica_groups=mesh['wide'=8,'narrow'=4] {'narrow','wide'}, dimensions={0} | all-to-all | bytes 294912 | tf_op jit(solution)/shard_map/all_to_all | solution.py:798
  169.3 6.1 %shard_map.157 = (f32[512,512]{1,0:T(8,128)S(1)}, f32[512,512]{1,0:T(8,128)S(1)}, f32[1,128]{1,0:T(1,128)S(1)}, f32[32,1,128]{2,1,0:T(1,128)S(1)}, f32[512,512]{1,0:T(8,128)S(1)}, /*index=5*/f32[512,512]{1,0:T(8,128)S(1)}) custom-call(f32[32,1,1152]{2,1,0:T(1,128)S(1)} %all_to_all.51.r_0_, f32[512,512]{1,0:T(8,128)S(1)} %get-tuple-element.86.r_1_, ...), custom_call_target="tpu_custom_call" | custom-call | flops 1000000000 | bytes 4194304 | tf_op jit(solution)/shard_map/pallas_call | solution.py:98
  175.4 9.6 %all_to_all.52.r_1_ = f32[32,1,128]{2,1,0:T(1,128)S(1)} all-to-all(f32[32,1,128]{2,1,0:T(1,128)S(1)} %get-tuple-element.97), channel_id=1, replica_groups=mesh['wide'=8,'narrow'=4] {'narrow','wide'}, dimensions={0} | all-to-all | bytes 32768 | tf_op jit(solution)/shard_map/all_to_all | solution.py:798
  185.0 0.4 shard_map.158
  185.4 52.9 %all_to_all.53.r_0_ = f32[8,528,128]{2,1,0:T(8,128)S(1)} all-to-all(f32[8,528,128]{2,1,0:T(8,128)S(1)} %shard_map.158), channel_id=1, replica_groups=mesh['wide'=8,'narrow'=4] {'wide'}, dimensions={0} | all-to-all | bytes 4325376 | tf_op jit(solution)/shard_map/all_to_all | solution.py:853
  238.4 3.9 %shard_map.159 = (f32[4,128,512]{2,1,0:T(8,128)}, f32[4,128,512]{2,1,0:T(8,128)}, f32[4,128,512]{2,1,0:T(8,128)}) custom-call(f32[8,528,128]{2,1,0:T(8,128)S(1)} %all_to_all.53.r_0_, f32[2,128,512]{2,1,0:T(8,128)S(1)} %get-tuple-element.103.r_1_, f32[2,128,512]{2,1,0:T(8,128)S(1)} %get-tuple-element.104.r_2_, f32[4,128,512]{2,1,0:T(8,128)S(1)} %get-tuple-element.105.r_3_), custom_call_target="tpu_custom_call" | custom-call | flops 1000000000 | bytes 4194304 | tf_op jit(solution)/shard_map/pallas_call | solution.py:98
  (23 shorter events, 0.1 us)
Async XLA Ops:
  0.6 1.2 copy-start.6
  1.9 1.2 copy-start.7
  3.1 0.7 copy-start.8
  4.1 56.9 %copy-start.10 = (f32[32,512]{1,0:T(8,128)S(1)}, f32[32,512]{1,0:T(8,128)}, u32[]{:S(2)}) copy-start(f32[32,512]{1,0:T(8,128)} %constant.20.clone.r_1_) | copy-start | bytes 196612
  61.0 12.1 %copy-start.4 = (f32[128,128]{1,0:T(8,128)S(1)}, f32[128,128]{1,0:T(8,128)}, u32[]{:S(2)}) copy-start(f32[128,128]{1,0:T(8,128)} %r_4_.7) | copy-start | bytes 196612
  61.0 12.1 %copy-start.5 = (f32[16,16]{1,0:T(8,128)S(1)}, f32[16,16]{1,0:T(8,128)}, u32[]{:S(2)}) copy-start(f32[16,16]{1,0:T(8,128)} %r_3_.7) | copy-start | bytes 3076
  61.3 15.2 %copy-start = (f32[512,512]{1,0:T(8,128)S(1)}, f32[512,512]{1,0:T(8,128)}, u32[]{:S(2)}) copy-start(f32[512,512]{1,0:T(8,128)} %constant.16.clone.r_6_.r_5_) | copy-start | bytes 3145732
  61.3 15.2 %copy-start.1 = (f32[2,256,256]{2,1,0:T(8,128)S(1)}, f32[2,256,256]{2,1,0:T(8,128)}, u32[]{:S(2)}) copy-start(f32[2,256,256]{2,1,0:T(8,128)} %constant.17.clone.r_5_.r_4_) | copy-start | bytes 1572868
  61.3 15.1 %collective-permute-start = (f32[64,512]{1,0:T(8,128)S(1)}, f32[64,512]{1,0:T(8,128)S(1)}, u32[]{:S(2)}, u32[]{:S(2)}) collective-permute-start(f32[64,512]{1,0:T(8,128)S(1)} %get-tuple-element.57), channel_id=1, source_target_pairs={{0,4},{4,8},{8,12},{12,16},{16,20},{20,24},{24,28},{28,29},{29,25}... | collective-permute-start | bytes 393224 | tf_op jit(solution)/shard_map/ppermute | solution.py:725
  64.0 12.4 %collective-permute-start.1 = (f32[64,512]{1,0:T(8,128)S(1)}, f32[64,512]{1,0:T(8,128)S(1)}, u32[]{:S(2)}, u32[]{:S(2)}) collective-permute-start(f32[64,512]{1,0:T(8,128)S(1)} %get-tuple-element.58), channel_id=1, source_target_pairs={{4,0},{8,4},{12,8},{16,12},{20,16},{24,20},{28,24},{29,28},{25,29}... | collective-permute-start | bytes 393224 | tf_op jit(solution)/shard_map/ppermute | solution.py:726
  65.3 4.8 %collective-permute-start.2 = (f32[2,4,1,512]{3,2,1,0:T(1,128)S(1)}, f32[2,4,1,512]{3,2,1,0:T(1,128)S(1)}, u32[]{:S(2)}, u32[]{:S(2)}) collective-permute-start(f32[2,4,1,512]{3,2,1,0:T(1,128)S(1)} %get-tuple-element.59), channel_id=1, source_target_pairs={{0,1},{1,2},{2,3},{4,5},{5,6},{6,7},{8,9},{9,10},{10,11},{12,13},{... | collective-permute-start | bytes 49160 | tf_op jit(solution)/shard_map/ppermute | solution.py:730
  68.8 4.3 %collective-permute-start.3 = (f32[2,4,1,512]{3,2,1,0:T(1,128)S(1)}, f32[2,4,1,512]{3,2,1,0:T(1,128)S(1)}, u32[]{:S(2)}, u32[]{:S(2)}) collective-permute-start(f32[2,4,1,512]{3,2,1,0:T(1,128)S(1)} %get-tuple-element.60), channel_id=1, source_target_pairs={{1,0},{2,1},{3,2},{5,4},{6,5},{7,6},{9,8},{10,9},{11,10},{13,12},{... | collective-permute-start | bytes 49160 | tf_op jit(solution)/shard_map/ppermute | solution.py:731
  76.4 22.1 %copy-start.9 = (f32[32,2,512]{2,1,0:T(2,128)S(1)}, f32[32,2,512]{2,1,0:T(2,128)}, u32[]{:S(2)}) copy-start(f32[32,2,512]{2,1,0:T(2,128)} %constant.21.clone.r_3_) | copy-start | bytes 393220
  76.5 22.1 %copy-start.11 = (f32[32,128]{1,0:T(8,128)S(1)}, f32[32,128]{1,0:T(8,128)}, u32[]{:S(2)}) copy-start(f32[32,128]{1,0:T(8,128)} %constant.23.clone.r_5_) | copy-start | bytes 49156
  76.5 22.1 %copy-start.12 = (f32[32,32]{1,0:T(8,128)S(1)}, f32[32,32]{1,0:T(8,128)}, u32[]{:S(2)}) copy-start(f32[32,32]{1,0:T(8,128)} %constant.22.clone.r_4_) | copy-start | bytes 12292
  85.7 23.6 %copy-start.2 = (f32[2,256,256]{2,1,0:T(8,128)S(1)}, f32[2,256,256]{2,1,0:T(8,128)}, u32[]{:S(2)}) copy-start(f32[2,256,256]{2,1,0:T(8,128)} %constant.18.clone.r_3_) | copy-start | bytes 1572868
  85.8 23.6 %copy-start.3 = (f32[64,64]{1,0:T(8,128)S(1)}, f32[64,64]{1,0:T(8,128)}, u32[]{:S(2)}) copy-start(f32[64,64]{1,0:T(8,128)} %constant.19.clone.r_6_) | copy-start | bytes 49156
